TPU v7x, 32 devices: a whole 2x2x4 slice. The times are simulated.
32 devices in a mesh: rep: 4 (over y, core), gx: 4 (over z), gy: 2 (over x).
Axes of the slice: x: 2, y: 2, z: 4, core: 2. Of those that a mesh axis runs over, the one named last changes fastest.
Arguments:
- hidden_one: bfloat16 [512, 8192], P(('rep', 'gy'), 'gx'), may hold values from -6 to 6
- hidden_two: bfloat16 [512, 8192], P(('rep', 'gy'), 'gx'), may hold values from -6 to 6
- w_qkv: bfloat16 [8192, 10240], P('gx', 'gy'), may hold values from -0.0625 to 0.0625
- w_out: bfloat16 [8192, 8192], P('gy', 'gx'), may hold values from -0.0625 to 0.0625
- key_cache: bfloat16 [512, 128, 1024], P(('rep', 'gx'), None, 'gy'), may hold values from -1000 to 1000
- value_cache: bfloat16 [512, 128, 1024], P(('rep', 'gx'), None, 'gy'), may hold values from -6 to 6
- lengths: int32 [4, 128], P(None, 'gx'), may hold values from 1 to 126, 8064 in all within a row
- mig_rows: int32 [4, 8, 2], P(None, 'gx'), may hold values from 0 to 15, as said below
- dest: int32 [4, 8, 2], P(None, 'gx'), may hold values from 0 to 3, as said below
Outputs:
- out_one: bfloat16 [512, 8192], P(('rep', 'gy'), 'gx')
- out_two: bfloat16 [512, 8192], P(('rep', 'gy'), 'gx')
Inputs may be any that keep to these rules, and one draw needn't show every extreme that they name: mig_rows[r, p, :] are distinct; rows p * 16 + mig_rows[r, p, k] of replica r leave. For every block p and slot k, dest[:, p, k] names every replica once; the entries of dest[r, p, :] are distinct. The 128 lengths of each replica sum to 8064.
All inputs are finite; a program needn't handle non-finite values. No bound on the sum of `lengths` on one device may be relied on, other than what follows from the above.
Results may differ from a plain program's by a relative error of at most 0.015.
Values may be sent and summed in bfloat16 or wider, within the bound.
No kernel may reach another device: no remote copies, remote signals or barrier semaphores. Data moves between devices by JAX's collectives and lax.ppermute only.
A program may use at most 128 MiB of HBM per device.

v0:
```python
import math

import jax
import jax.numpy as jnp
from jax import lax
from jax.sharding import PartitionSpec as P

HEADS = 64
KV_HEADS = 8
HEAD_DIM = 128
ROWS_DEV = 16
MIG_DEV = 2


ROPE_BASE = 500000.0


def rotate(vectors, positions):
    half_dim = vectors.shape[-1] // 2
    inverse = ROPE_BASE ** (-(jnp.arange(half_dim, dtype=jnp.float32) * 2.0 / vectors.shape[-1]))
    angles = positions.astype(jnp.float32)[:, None, None] * inverse[None, None, :]
    cosine = jnp.cos(angles)
    sine_part = jnp.sin(angles)
    first_half = vectors[..., :half_dim]
    second_half = vectors[..., half_dim:]
    return jnp.concatenate(
        [
            first_half * cosine - second_half * sine_part,
            second_half * cosine + first_half * sine_part,
        ],
        axis=-1,
    )


def project_rows(hidden, w_qkv, positions):
    row_count = positions.shape[0]
    group_size = HEADS // KV_HEADS
    gathered = lax.all_gather(hidden, "gy", axis=0, tiled=True)
    totals = lax.psum_scatter(
        jnp.dot(gathered, w_qkv, preferred_element_type=jnp.float32),
        "gx",
        scatter_dimension=0,
        tiled=True,
    )
    totals = totals.reshape(row_count, -1, group_size + 2, HEAD_DIM)
    local_groups = totals.shape[1]
    queries = rotate(
        totals[:, :, :group_size].reshape(row_count, local_groups * group_size, HEAD_DIM), positions
    ).astype(jnp.bfloat16)
    new_keys = rotate(totals[:, :, group_size], positions)
    new_keys = new_keys.reshape(row_count, local_groups * HEAD_DIM).astype(jnp.bfloat16)
    new_values = (
        totals[:, :, group_size + 1]
        .reshape(row_count, local_groups * HEAD_DIM)
        .astype(jnp.bfloat16)
    )
    return (queries, new_keys, new_values)


def cache_part(queries, cache_keys, cache_values, live_count):
    row_count = queries.shape[0]
    slot_count = cache_keys.shape[1]
    score_scale = 1.0 / math.sqrt(HEAD_DIM)
    grouped = queries.reshape(row_count, -1, HEADS // KV_HEADS, HEAD_DIM)
    keys_split = cache_keys.reshape(row_count, slot_count, -1, HEAD_DIM)
    values_split = cache_values.reshape(row_count, slot_count, -1, HEAD_DIM)
    scores = (
        jnp.einsum("ngjd,nsgd->ngjs", grouped, keys_split, preferred_element_type=jnp.float32)
        * score_scale
    )
    live_mask = (jnp.arange(slot_count, dtype=jnp.int32)[None, :] < live_count[:, None])[
        :, None, None, :
    ]
    highest = jnp.max(jnp.where(live_mask, scores, -jnp.inf), axis=-1)
    weights = jnp.where(live_mask, jnp.exp(scores - highest[..., None]), 0.0)
    weight_sum = jnp.sum(weights, axis=-1)
    blended = jnp.einsum(
        "ngjs,nsgd->ngjd",
        weights.astype(jnp.bfloat16),
        values_split,
        preferred_element_type=jnp.float32,
    )
    return (blended, highest, weight_sum)


def finish(queries, partial_value, new_keys, new_values):
    blended, highest, weight_sum = partial_value
    row_count = queries.shape[0]
    score_scale = 1.0 / math.sqrt(HEAD_DIM)
    grouped = queries.reshape(row_count, -1, HEADS // KV_HEADS, HEAD_DIM)
    fresh_keys = new_keys.reshape(row_count, -1, HEAD_DIM)
    fresh_score = (
        jnp.einsum("ngjd,ngd->ngj", grouped, fresh_keys, preferred_element_type=jnp.float32)
        * score_scale
    )
    joint_max = jnp.maximum(highest, fresh_score)
    old_share = jnp.exp(highest - joint_max)
    new_share = jnp.exp(fresh_score - joint_max)
    fresh_values = new_values.reshape(row_count, -1, 1, HEAD_DIM).astype(jnp.float32)
    merged = (old_share[..., None] * blended + new_share[..., None] * fresh_values) / (
        old_share * weight_sum + new_share
    )[..., None]
    return merged.reshape(row_count, -1).astype(jnp.bfloat16)


def mix_out(attended, w_out):
    partial_out = jnp.dot(
        lax.all_gather(attended, "gx", axis=0, tiled=True),
        w_out,
        preferred_element_type=jnp.float32,
    )
    return lax.psum_scatter(partial_out.astype(jnp.bfloat16), "gy", scatter_dimension=0, tiled=True)


def spread(hit_table, member):
    widened = hit_table.reshape(hit_table.shape + (1,) * (member.ndim - 1))
    return jnp.where(widened, member[None], jnp.zeros((), member.dtype))


def body(hidden_one, hidden_two, w_qkv, w_out, key_cache, value_cache, lengths, mig_rows, dest):
    replica = lax.axis_index("rep")
    replicas = lax.axis_size("rep")
    own_lengths = lengths[replica]
    query_one, key_one, value_one = project_rows(hidden_one, w_qkv, own_lengths)
    attended_one = finish(
        query_one, cache_part(query_one, key_cache, value_cache, own_lengths), key_one, value_one
    )
    out_one = mix_out(attended_one, w_out)
    slot_ids = jnp.arange(key_cache.shape[1], dtype=jnp.int32)
    written = (slot_ids[None, :] == own_lengths[:, None])[:, :, None]
    keys_one = jnp.where(written, key_one[:, None, :], key_cache)
    values_one = jnp.where(written, value_one[:, None, :], value_cache)
    live_one = own_lengths + 1
    blocks_here = mig_rows.shape[1]
    block_base = jnp.arange(blocks_here, dtype=jnp.int32)[:, None] * ROWS_DEV + jnp.zeros(
        (1, MIG_DEV), jnp.int32
    )
    block_base = block_base.reshape(-1)
    mig_flat = mig_rows.reshape(mig_rows.shape[0], -1)
    leaving = block_base + mig_flat[replica]
    heading = dest[replica].reshape(-1)
    replica_ids = jnp.arange(replicas, dtype=jnp.int32)
    came_from = jnp.sum(
        replica_ids[:, None, None] * (dest == replica).astype(jnp.int32), axis=0
    ).reshape(-1)
    slot_order = jnp.arange(leaving.shape[0], dtype=jnp.int32)
    source_rows = block_base + mig_flat[came_from, slot_order]
    arrive_live = lengths[came_from, source_rows] + 1
    row_ids = jnp.arange(own_lengths.shape[0], dtype=jnp.int32)
    landing_hit = row_ids[:, None] == leaving[None, :]
    arrived = jnp.any(landing_hit, axis=1)
    pick = jnp.sum(jnp.where(landing_hit, slot_order[None, :], 0), axis=1)
    live_two = jnp.where(arrived, arrive_live[pick], live_one)
    query_two, key_two, value_two = project_rows(hidden_two, w_qkv, live_two)
    send_hit = replica_ids[:, None] == heading[None, :]

    def place(table, arrivals):
        row_mask = arrived.reshape((table.shape[0],) + (1,) * (table.ndim - 1))
        return jnp.where(row_mask, arrivals[pick], table)

    got_keys, got_values = (
        lax.all_to_all(
            spread(send_hit, keys_one[leaving]), "rep", split_axis=0, concat_axis=0, tiled=True
        ),
        lax.all_to_all(
            spread(send_hit, values_one[leaving]), "rep", split_axis=0, concat_axis=0, tiled=True
        ),
    )
    keys_two = place(keys_one, got_keys[came_from, slot_order])
    values_two = place(values_one, got_values[came_from, slot_order])
    partial_value = cache_part(query_two, keys_two, values_two, live_two)
    attended_two = finish(query_two, partial_value, key_two, value_two)
    out_two = mix_out(attended_two, w_out)
    return (out_one, out_two)


def solution(mesh):
    placed = (
        P(("rep", "gy"), "gx"),
        P(("rep", "gy"), "gx"),
        P("gx", "gy"),
        P("gy", "gx"),
        P(("rep", "gx"), None, "gy"),
        P(("rep", "gx"), None, "gy"),
        P(None, "gx"),
        P(None, "gx", None),
        P(None, "gx", None),
    )
    return jax.shard_map(
        body,
        mesh=mesh,
        in_specs=placed,
        out_specs=(P(("rep", "gy"), "gx"), P(("rep", "gy"), "gx")),
        check_vma=False,
    )
```

profile of v0, /device:TPU:0, one launch (start us, length us, event | category | flops | bytes accessed | tf_op | source)
XLA Modules:
  0.0 259.2 jit_solution(16048945605678223815)
XLA Ops:
  7.2 10.2 %all_gather.12 = bf16[128,2048]{1,0:T(8,128)(2,1)S(1)} all-gather(bf16[64,2048]{1,0:T(8,128)(2,1)} %param.9), channel_id=1, replica_groups=mesh['rep'=4,'gx'=4,'gy'=2] {'gy'}, dimensions={0}, use_global_device_ids=true | all-gather | bytes 786432 | tf_op jit(solution)/shard_map/all_gather | solution.py:38
  17.4 11.4 %fusion.95 = f32[128,5120]{1,0:T(8,128)} fusion(bf16[128,2048]{1,0:T(8,128)(2,1)S(1)} %all_gather.12, bf16[2048,5120]{1,0:T(8,128)(2,1)} %param.11), kind=kOutput, calls=%fused_computation.143 | convolution fusion | flops 2684354560 | bytes 24117248 | tf_op jit(solution)/shard_map/dot_general | solution.py:40
  29.0 8.1 %all_gather.14 = bf16[128,2048]{1,0:T(8,128)(2,1)S(1)} all-gather(bf16[64,2048]{1,0:T(8,128)(2,1)S(1)} %copy-done.5), channel_id=1, replica_groups=mesh['rep'=4,'gx'=4,'gy'=2] {'gy'}, dimensions={0}, use_global_device_ids=true | all-gather | bytes 786432 | tf_op jit(solution)/shard_map/all_gather | solution.py:38
  37.1 11.5 %fusion.96 = f32[128,5120]{1,0:T(8,128)} fusion(bf16[128,2048]{1,0:T(8,128)(2,1)S(1)} %all_gather.14, bf16[2048,5120]{1,0:T(8,128)(2,1)} %param.11), kind=kOutput, calls=%fused_computation.144 | convolution fusion | flops 2684354560 | bytes 24117248 | tf_op jit(solution)/shard_map/dot_general | solution.py:40
  49.1 0.2 dynamic-slice_reduce_fusion
  49.4 0.6 gather_fusion
  50.3 0.6 gather_fusion.1
  50.9 0.7 fusion.94
  51.8 2.5 fusion.89
  54.5 0.2 multiply_cosine_fusion
  54.7 28.1 %reduce-scatter.5.cloned.1.call-done = f32[32,5120]{1,0:T(8,128)} async-done(((f32[128,5120]{1,0:T(8,128)}), f32[32,5120]{1,0:T(8,128)}) %reduce-scatter.5.cloned.1.call-update) | async-done | bytes 655376 | tf_op jit(solution)/shard_map/reduce_scatter | solution.py:39
  82.8 1.2 reshape.419
  84.3 0.2 fusion.67
  84.5 5.9 %broadcast_select_fusion.1 = (bf16[32,128,512]{2,1,0:T(8,128)(2,1)}, bf16[32,128,512]{2,1,0:T(8,128)(2,1)}) fusion(bf16[32,128,512]{2,1,0:T(8,128)(2,1)} %param.13, pred[32,128]{1,0:T(8,128)(4,1)S(1)} %get-tuple-element.35, bf16[32,512]{1,0:T(8,128)(2,1)S(1)} %get-tuple-element.49, bf16[32,128,512]{2,1,0:T(8,128)(2,1)} %param.14, ...), kind=kLoop, calls=%fused_computation.23 | loop fusion | flops 4194304 | bytes 16846848 | tf_op jit(solution)/shard_map/jit(_where)/select_n | solution.py:131
  90.4 2.9 %gather_fusion.2 = bf16[4,128,512]{2,1,0:T(8,128)(2,1)S(1)} fusion(bf16[32,128,512]{2,1,0:T(8,128)(2,1)} %get-tuple-element.21, s32[1024]{0:T(1024)S(1)} %pad_clamp_fusion.1), kind=kCustom, calls=%fused_computation.2 | custom fusion | bytes 1048592 | tf_op jit(solution)/shard_map/gather | solution.py:163
  93.3 2.8 %gather_fusion.5 = bf16[4,128,512]{2,1,0:T(8,128)(2,1)S(1)} fusion(bf16[32,128,512]{2,1,0:T(8,128)(2,1)} %get-tuple-element.22, s32[1024]{0:T(1024)S(1)} %pad_clamp_fusion.1), kind=kCustom, calls=%fused_computation.5 | custom fusion | bytes 1048592 | tf_op jit(solution)/shard_map/gather | solution.py:166
  96.1 2.3 broadcast_select_fusion.3
  98.4 3.6 %all-to-all-start.1 = ((bf16[4,4,128,512]{3,2,1,0:T(8,128)(2,1)}), bf16[4,4,128,512]{3,2,1,0:T(8,128)(2,1)S(1)}, u32[]{:S(2)}, u32[]{:S(2)}) async-start(bf16[4,4,128,512]{3,2,1,0:T(8,128)(2,1)} %get-tuple-element.32), calls=%async_computation.4 | async-start | bytes 4194304 | tf_op jit(solution)/shard_map/all_to_all | solution.py:165
  102.1 34.8 %reduce-scatter.9.cloned.1.call-done = f32[32,5120]{1,0:T(8,128)} async-done(((f32[128,5120]{1,0:T(8,128)}), f32[32,5120]{1,0:T(8,128)}) %reduce-scatter.9.cloned.1.call-update) | async-done | bytes 655376 | tf_op jit(solution)/shard_map/reduce_scatter | solution.py:39
  136.9 2.3 reshape.427
  139.3 1.2 slice_bitcast_fusion.1
  140.5 1.2 slice_bitcast_fusion
  141.7 0.5 fusion.48
  142.2 0.3 fusion.65
  142.6 2.4 select_reduce_fusion.1
  145.0 4.5 %all-to-all-start = ((bf16[4,4,128,512]{3,2,1,0:T(8,128)(2,1)}), bf16[4,4,128,512]{3,2,1,0:T(8,128)(2,1)}, u32[]{:S(2)}, u32[]{:S(2)}) async-start(bf16[4,4,128,512]{3,2,1,0:T(8,128)(2,1)} %get-tuple-element.31), calls=%async_computation.3 | async-start | bytes 4194304 | tf_op jit(solution)/shard_map/all_to_all | solution.py:162
  149.5 0.2 all-gather.3.cloned.1.call-start
  149.7 0.4 fusion.42
  150.1 1.1 slice.88
  151.3 3.5 %fusion.39 = bf16[32,4,8,128]{3,2,1,0:T(8,128)(2,1)S(1)} fusion(f32[32,4,8,128]{3,2,1,0:T(8,128)S(1)} %get-tuple-element.42, f32[32,4,8]{2,1,0:T(4,128)S(1)} %get-tuple-element.8, f32[32,4,128]{2,1,0:T(4,128)S(1)} %bitcast.142, f32[32,4,8]{2,1,0:T(4,128)S(1)} %get-tuple-element.10, f32[32,4,8]{2,1,0:T(4,128)S(1)} %get-tuple-element.41, ...), kind=kOutput, calls=%fused_computation.37 | convolution fusion | flops 34603008 | bytes 5066752 | tf_op jit(solution)/shard_map/ngjs,nsgd->ngjd/dot_general | solution.py:77
  154.8 0.8 copy.88
  155.9 0.3 fusion.63
  156.2 1.1 fusion.62
  157.3 0.6 gather_fusion.6
  157.9 2.8 %gather_fusion.7 = bf16[32,128,512]{2,1,0:T(8,128)(2,1)} fusion(bf16[4,128,512]{2,1,0:T(8,128)(2,1)S(1)} %gather_fusion.6, s32[1024]{0:T(1024)S(1)} %pad_clamp_fusion), kind=kCustom, calls=%fused_computation.7 | custom fusion | bytes 8388736 | tf_op jit(solution)/shard_map/gather | solution.py:159
  160.7 14.5 %all-to-all-done = bf16[4,4,128,512]{3,2,1,0:T(8,128)(2,1)} async-done(((bf16[4,4,128,512]{3,2,1,0:T(8,128)(2,1)}), bf16[4,4,128,512]{3,2,1,0:T(8,128)(2,1)}, u32[]{:S(2)}, u32[]{:S(2)}) %all-to-all-start) | async-done | bytes 2097184 | tf_op jit(solution)/shard_map/all_to_all | solution.py:162
  175.2 2.2 gather_fusion.3
  177.4 2.8 %gather_fusion.4 = bf16[32,128,512]{2,1,0:T(8,128)(2,1)} fusion(bf16[4,128,512]{2,1,0:T(8,128)(2,1)S(1)} %gather_fusion.3, s32[1024]{0:T(1024)S(1)} %pad_clamp_fusion), kind=kCustom, calls=%fused_computation.4 | custom fusion | bytes 8388736 | tf_op jit(solution)/shard_map/gather | solution.py:159
  180.1 6.3 %select_bitcast_fusion.1 = (bf16[32,16,4,8,128]{4,3,2,1,0:T(8,128)(2,1)S(1)}, bf16[32,16,4,8,128]{4,3,2,1,0:T(8,128)(2,1)S(1)}) fusion(bf16[32,128,512]{2,1,0:T(8,128)(2,1)} %gather_fusion.4, bf16[32,128,512]{2,1,0:T(8,128)(2,1)} %get-tuple-element.21, pred[32]{0:T(512)(128)(4,1)S(1)} %fusion.70, bf16[32,128,512]{2,1,0:T(8,128)(2,1)} %gather_fusion.7, ...), kind=kLoop, calls=%fused_computation.21 | loop fusion | flops 4194304 | bytes 25165856
  186.5 2.4 select_reduce_fusion
  188.9 0.5 fusion.44
  189.4 1.3 fusion.33
  190.7 0.8 copy.87
  191.6 9.4 %convolution_convert_fusion.1 = bf16[128,2048]{1,0:T(8,128)(2,1)} fusion(bf16[128,4096]{1,0:T(8,128)(2,1)} %all-gather.3.cloned.1.call-done, bf16[4096,2048]{1,0:T(8,128)(2,1)} %param.12), kind=kOutput, calls=%fused_computation.25 | convolution fusion | flops 2147745792 | bytes 18350080 | tf_op jit(solution)/shard_map/dot_general | solution.py:107
  201.1 17.3 %all-gather.5.cloned.1.call-done = bf16[128,4096]{1,0:T(8,128)(2,1)} async-done(((bf16[32,4096]{1,0:T(8,128)(2,1)}), bf16[128,4096]{1,0:T(8,128)(2,1)}) %all-gather.5.cloned.1.call-update) | async-done | bytes 1048592 | tf_op jit(solution)/shard_map/all_gather | solution.py:108
  218.4 9.3 %convolution_convert_fusion = bf16[128,2048]{1,0:T(8,128)(2,1)} fusion(bf16[128,4096]{1,0:T(8,128)(2,1)} %all-gather.5.cloned.1.call-done, bf16[4096,2048]{1,0:T(8,128)(2,1)} %param.12), kind=kOutput, calls=%fused_computation.24 | convolution fusion | flops 2147745792 | bytes 18350080 | tf_op jit(solution)/shard_map/dot_general | solution.py:107
  227.6 7.4 %reduce-scatter.7.cloned.1.call-done = bf16[64,2048]{1,0:T(8,128)(2,1)} async-done(((bf16[128,2048]{1,0:T(8,128)(2,1)}), bf16[64,2048]{1,0:T(8,128)(2,1)}) %reduce-scatter.7.cloned.1.call-update) | async-done | bytes 262160 | tf_op jit(solution)/shard_map/reduce_scatter | solution.py:112
  235.1 17.3 %reduce-scatter.11.cloned.1.call-done = bf16[64,2048]{1,0:T(8,128)(2,1)} async-done(((bf16[128,2048]{1,0:T(8,128)(2,1)}), bf16[64,2048]{1,0:T(8,128)(2,1)}) %reduce-scatter.11.cloned.1.call-update) | async-done | bytes 262160 | tf_op jit(solution)/shard_map/reduce_scatter | solution.py:112
  (58 shorter events, 2.1 us)
Async XLA Ops:
  7.2 42.2 %copy-start = (s32[4,2,2]{0,2,1:T(2,128)S(1)}, s32[4,2,2]{0,2,1:T(2,128)}, u32[]{:S(2)}) copy-start(s32[4,2,2]{0,2,1:T(2,128)} %param.16) | copy-start | bytes 196
  7.2 75.6 %reduce-scatter.5.cloned.1.call-start = ((), (), s32[]{:S(2)}) async-start(), calls=%async_computation.6 | async-start | bytes 3276800 | tf_op jit(solution)/shard_map/reduce_scatter | solution.py:39
  17.4 11.5 %copy-start.5 = (bf16[64,2048]{1,0:T(8,128)(2,1)S(1)}, bf16[64,2048]{1,0:T(8,128)(2,1)}, u32[]{:S(2)}) copy-start(bf16[64,2048]{1,0:T(8,128)(2,1)} %param.10) | copy-start | bytes 786436
  28.9 108.0 %reduce-scatter.9.cloned.1.call-start = ((), (), s32[]{:S(2)}) async-start(), calls=%async_computation.9 | async-start | bytes 3276800 | tf_op jit(solution)/shard_map/reduce_scatter | solution.py:39
  37.1 11.8 %copy-start.6 = (s32[4,2,2]{0,2,1:T(2,128)S(1)}, s32[4,2,2]{0,2,1:T(2,128)}, u32[]{:S(2)}) copy-start(s32[4,2,2]{0,2,1:T(2,128)} %param.17) | copy-start | bytes 196
  37.1 13.1 %copy-start.2 = (s32[4,32]{1,0:T(4,128)S(1)}, s32[4,32]{1,0:T(4,128)}, u32[]{:S(2)}) copy-start(s32[4,32]{1,0:T(4,128)} %param.15) | copy-start | bytes 1540
  84.0 6.4 %copy-start.4 = (f32[32,4,10,128]{3,2,1,0:T(8,128)}, f32[32,4,10,128]{3,2,1,0:T(8,128)S(1)}, u32[]{:S(2)}) copy-start(f32[32,4,10,128]{3,2,1,0:T(8,128)S(1)} %reshape.419) | copy-start | bytes 1966084
  98.4 46.5 %all-to-all-start.1 = ((bf16[4,4,128,512]{3,2,1,0:T(8,128)(2,1)}), bf16[4,4,128,512]{3,2,1,0:T(8,128)(2,1)S(1)}, u32[]{:S(2)}, u32[]{:S(2)}) async-start(bf16[4,4,128,512]{3,2,1,0:T(8,128)(2,1)} %get-tuple-element.32), calls=%async_computation.4 | async-start | bytes 4194304 | tf_op jit(solution)/shard_map/all_to_all | solution.py:165
  139.2 3.4 %copy-start.3 = (bf16[32,128,512]{2,1,0:T(8,128)(2,1)S(1)}, bf16[32,128,512]{2,1,0:T(8,128)(2,1)}, u32[]{:S(2)}) copy-start(bf16[32,128,512]{2,1,0:T(8,128)(2,1)} %param.13) | copy-start | bytes 12582916
  145.0 30.2 %all-to-all-start = ((bf16[4,4,128,512]{3,2,1,0:T(8,128)(2,1)}), bf16[4,4,128,512]{3,2,1,0:T(8,128)(2,1)}, u32[]{:S(2)}, u32[]{:S(2)}) async-start(bf16[4,4,128,512]{3,2,1,0:T(8,128)(2,1)} %get-tuple-element.31), calls=%async_computation.3 | async-start | bytes 4194304 | tf_op jit(solution)/shard_map/all_to_all | solution.py:162
  149.5 42.2 %all-gather.3.cloned.1.call-start = ((), (), s32[]{:S(2)}) async-start(), calls=%async_computation.7 | async-start | bytes 1310720 | tf_op jit(solution)/shard_map/all_gather | solution.py:108
  155.6 62.8 %all-gather.5.cloned.1.call-start = ((), (), s32[]{:S(2)}) async-start(), calls=%async_computation.10 | async-start | bytes 1310720 | tf_op jit(solution)/shard_map/all_gather | solution.py:108
  191.6 43.5 %reduce-scatter.7.cloned.1.call-start = ((), (), s32[]{:S(2)}) async-start(), calls=%async_computation.8 | async-start | bytes 786432 | tf_op jit(solution)/shard_map/reduce_scatter | solution.py:112
  201.0 51.4 %reduce-scatter.11.cloned.1.call-start = ((), (), s32[]{:S(2)}) async-start(), calls=%async_computation.11 | async-start | bytes 786432 | tf_op jit(solution)/shard_map/reduce_scatter | solution.py:112
  218.4 34.0 %copy-start.1 = (s32[4,2,2]{0,2,1:T(2,128)S(1)}, s32[4,2,2]{0,2,1:T(2,128)}, u32[]{:S(2)}) copy-start(s32[4,2,2]{0,2,1:T(2,128)} %param.16) | copy-start | bytes 196
Sparse Core Ops, SparseCore 0:
  29.0 53.6 reduce-scatter.4
  85.1 51.7 reduce-scatter.8
  155.7 27.7 all-gather.2
  191.7 26.6 all-gather.4
  221.0 13.9 reduce-scatter.6
  237.7 14.6 reduce-scatter.10
where the time goes:
time: 260 us; the launch traced here: 259 us
  waiting for transfers between devices  120 us (46%)
  matrix products  51.8 us (20%)
  local copies, waits for them, and re-layouts  25.4 us (10%)
  other arithmetic  21.2 us (8%)
  blocking collectives  18.3 us (7%)
  between operations  14.4 us (6%)
  starting transfers between devices  8.51 us (3%)
    reduce_scatter x2, waiting for transfers between devices, project_rows(): lax.psum_scatter(jnp.dot(gathered, w_qkv, preferred_element_type=jnp.floa...  62.9 us
    reduce_scatter x2, waiting for transfers between devices, mix_out(): lax.psum_scatter(partial_out.astype(jnp.bfloat16), 'gy', scatter_dimensio...  24.8 us
    dot_general x2, matrix products, project_rows(): jnp.dot(gathered, w_qkv, preferred_element_type=jnp.float32)  22.9 us
    dot_general x2, matrix products, mix_out(): jnp.dot(lax.all_gather(attended, 'gx', axis=0, tiled=True), w_out, prefer...  18.6 us
    all_gather x2, blocking collectives, project_rows(): gathered = lax.all_gather(hidden, 'gy', axis=0, tiled=True)  18.3 us
    all_gather x2, waiting for transfers between devices, mix_out(): lax.all_gather(attended, 'gx', axis=0, tiled=True)  17.3 us
    all_to_all x1, waiting for transfers between devices, body(): lax.all_to_all(spread(send_hit, keys_one[leaving]), 'rep', split_axis=0,...  14.5 us
    unnamed x1, other arithmetic  6.35 us
  transfers between devices with their start and end apart: 8, of which 6 were waited for; matrix products, arithmetic and copies ran while one was open for 34% of the time, Pallas kernels for 0%

commit v1 on v0

v1 whole, which is shorter than its diff:
```python
import math

import jax
import jax.numpy as jnp
from jax import lax
from jax.sharding import PartitionSpec as P

HEADS = 64
KV_HEADS = 8
HEAD_DIM = 128
ROWS_DEV = 16
GROUP = HEADS // KV_HEADS
ROPE_BASE = 500000.0
LINK_SCALE = 16.0
SCORE_SCALE = 1.0 / math.sqrt(HEAD_DIM)


def swap(value, axis, bit):
    count = lax.axis_size(axis)
    return lax.ppermute(value, axis, [(i, i ^ bit) for i in range(count)])


def power_of_two(count):
    return count & (count - 1) == 0


def gather_rows(hidden):
    if lax.axis_size("gy") != 2:
        return lax.all_gather(hidden, "gy", axis=0, tiled=True)
    peer = swap(hidden, "gy", 1)
    first = lax.axis_index("gy") == 0
    return jnp.concatenate([jnp.where(first, hidden, peer), jnp.where(first, peer, hidden)], axis=0)


def narrow(value):
    return (value * LINK_SCALE).astype(jnp.float16)


def widen(value):
    return value.astype(jnp.float32) * (1.0 / LINK_SCALE)


def project_sums(gathered, w_qkv):
    count = lax.axis_size("gx")
    if not power_of_two(count):
        return lax.psum_scatter(
            jnp.dot(gathered, w_qkv, preferred_element_type=jnp.float32),
            "gx", scatter_dimension=0, tiled=True,
        )
    place = lax.axis_index("gx")
    rows = gathered.shape[0] // count
    order = sorted(range(count), key=lambda k: [1 - (k >> b & 1) for b in range(count.bit_length() - 1)])
    blocks = [lax.dynamic_slice_in_dim(gathered, (place ^ k) * rows, rows, 0) for k in order]
    partial = jnp.dot(jnp.concatenate(blocks, axis=0), w_qkv, preferred_element_type=jnp.float32)
    bit = 1
    while bit < count:
        half = partial.shape[0] // 2
        received = swap(narrow(partial[:half]), "gx", bit)
        partial = partial[half:] + widen(received)
        bit *= 2
    return partial


def turn_tables(positions):
    half_dim = HEAD_DIM // 2
    inverse = ROPE_BASE ** (-(jnp.arange(half_dim, dtype=jnp.float32) * 2.0 / HEAD_DIM))
    angles = positions.astype(jnp.float32)[:, None] * inverse[None, :]
    return jnp.cos(angles), jnp.sin(angles)


def rotate(vectors, tables):
    half_dim = HEAD_DIM // 2
    cosine, sine = (t[:, None, None, :] for t in tables)
    first, second = vectors[..., :half_dim], vectors[..., half_dim:]
    return jnp.concatenate([first * cosine - second * sine, second * cosine + first * sine], axis=-1)


def split_sums(sums, tables):
    blocks = sums.reshape(sums.shape[0], -1, GROUP + 2, HEAD_DIM)
    turned = rotate(blocks[:, :, : GROUP + 1], tables).astype(jnp.bfloat16)
    return turned, blocks[:, :, GROUP + 1].astype(jnp.bfloat16)


def cache_part(queries, keys_split, values_split, live_count):
    slot_count = keys_split.shape[1]
    scores = jnp.einsum("ngjd,nsgd->ngjs", queries, keys_split, preferred_element_type=jnp.float32) * SCORE_SCALE
    live_mask = (jnp.arange(slot_count, dtype=jnp.int32)[None, :] < live_count[:, None])[:, None, None, :]
    highest = jnp.max(jnp.where(live_mask, scores, -jnp.inf), axis=-1)
    weights = jnp.where(live_mask, jnp.exp(scores - highest[..., None]), 0.0)
    weight_sum = jnp.sum(weights, axis=-1)
    blended = jnp.einsum(
        "ngjs,nsgd->ngjd", weights.astype(jnp.bfloat16), values_split, preferred_element_type=jnp.float32
    )
    return blended, highest, weight_sum


def attend(queries, keys_split, values_split, live_count, fresh):
    blended, highest, weight_sum = cache_part(queries, keys_split, values_split, live_count)
    wide = queries.astype(jnp.float32)
    scores = [
        jnp.sum(wide * key[:, :, None, :].astype(jnp.float32), axis=-1) * SCORE_SCALE for key, _ in fresh
    ]
    joint = highest
    for score in scores:
        joint = jnp.maximum(joint, score)
    share = jnp.exp(highest - joint)
    top = share[..., None] * blended
    bottom = share * weight_sum
    for score, (_, value) in zip(scores, fresh):
        share = jnp.exp(score - joint)
        top = top + share[..., None] * value[:, :, None, :].astype(jnp.float32)
        bottom = bottom + share
    return (top / bottom[..., None]).astype(jnp.bfloat16)


def mix_out(attended, w_out):
    count = lax.axis_size("gx")
    sides = lax.axis_size("gy")
    if not power_of_two(count) or sides != 2 or count % sides:
        partial = jnp.dot(
            lax.all_gather(attended, "gx", axis=0, tiled=True), w_out, preferred_element_type=jnp.float32
        )
        return lax.psum_scatter(partial.astype(jnp.bfloat16), "gy", scatter_dimension=0, tiled=True)
    place = lax.axis_index("gx")
    side = lax.axis_index("gy")
    rows = attended.shape[0]
    held, positions = attended, [0]
    bit = count // 2
    while bit:
        held = jnp.concatenate([held, swap(held, "gx", bit)], axis=0)
        positions = positions + [k ^ bit for k in positions]
        bit //= 2
    spots = jnp.zeros((count,), jnp.int32).at[jnp.array(positions)].set(jnp.arange(count, dtype=jnp.int32))
    share = count // sides

    def half_of(which):
        return jnp.concatenate(
            [
                lax.dynamic_slice_in_dim(held, spots[(which * share + j) ^ place] * rows, rows, 0)
                for j in range(share)
            ],
            axis=0,
        )

    lined = jnp.concatenate([half_of(1 - side), half_of(side)], axis=0)
    partial = jnp.dot(lined, w_out, preferred_element_type=jnp.float32)
    half = partial.shape[0] // 2
    received = swap(partial[:half].astype(jnp.bfloat16), "gy", 1)
    return (partial[half:] + received.astype(jnp.float32)).astype(jnp.bfloat16)


def trade(table, slots, partners):
    count = lax.axis_size("rep")
    replica = lax.axis_index("rep")
    own = table[slots]
    held = [own] + [
        lax.ppermute(own, "rep", [(i, (i + m) % count) for i in range(count)]) for m in range(1, count)
    ]
    away = jnp.mod(replica - partners, count)
    row_ids = jnp.arange(table.shape[0], dtype=jnp.int32)
    for s in range(slots.shape[0]):
        got = held[0][s]
        for m in range(1, count):
            got = jnp.where(away[s] == m, held[m][s], got)
        table = jnp.where((row_ids == slots[s])[:, None], got[None], table)
    return table


def body(hidden_one, hidden_two, w_qkv, w_out, key_cache, value_cache, lengths, mig_rows, dest):
    replica = lax.axis_index("rep")
    replicas = lax.axis_size("rep")
    own_lengths = lengths[replica]
    row_count = own_lengths.shape[0]
    blocks_here = mig_rows.shape[1]
    leave_each = mig_rows.shape[2]
    block_base = jnp.repeat(jnp.arange(blocks_here, dtype=jnp.int32) * ROWS_DEV, leave_each)
    mig_flat = mig_rows.reshape(replicas, -1)
    dest_flat = dest.reshape(replicas, -1)
    leaving = block_base + mig_flat[replica]
    heading = dest_flat[replica]
    replica_ids = jnp.arange(replicas, dtype=jnp.int32)
    came_from = jnp.sum(replica_ids[:, None] * (dest_flat == replica).astype(jnp.int32), axis=0)
    row_ids = jnp.arange(row_count, dtype=jnp.int32)
    from_hit = (row_ids[None, None, :] == (block_base[None] + mig_flat)[:, :, None]) & (
        replica_ids[:, None] == came_from[None]
    )[:, :, None]
    arrive_lengths = jnp.sum(jnp.where(from_hit, lengths[:, None, :], 0), axis=(0, 2))
    land_hit = row_ids[None, :] == leaving[:, None]
    lengths_two = jnp.where(
        jnp.any(land_hit, axis=0), jnp.sum(jnp.where(land_hit, arrive_lengths[:, None], 0), axis=0), own_lengths
    )
    tables_one = turn_tables(own_lengths)
    tables_two = turn_tables(lengths_two + 1)
    keys_split = key_cache.reshape(row_count, key_cache.shape[1], -1, HEAD_DIM)
    values_split = value_cache.reshape(row_count, value_cache.shape[1], -1, HEAD_DIM)
    groups = keys_split.shape[2]

    sums_one = project_sums(gather_rows(hidden_one), w_qkv)
    sums_two = project_sums(gather_rows(hidden_two), w_qkv)

    turned_one, value_one = split_sums(sums_one, tables_one)
    key_one = turned_one[:, :, GROUP]
    fresh_one = (key_one, value_one)
    attended_one = attend(turned_one[:, :, :GROUP], keys_split, values_split, own_lengths, (fresh_one,))
    out_one = mix_out(attended_one.reshape(row_count, -1), w_out)

    turned_two, value_two = split_sums(sums_two, tables_two)
    packed = jnp.concatenate([turned_two, value_two[:, :, None, :]], axis=2).reshape(row_count, -1)
    packed = trade(packed, leaving, heading).reshape(row_count, groups, GROUP + 2, HEAD_DIM)
    fresh_two = (packed[:, :, GROUP], packed[:, :, GROUP + 1])
    attended_two = attend(
        packed[:, :, :GROUP], keys_split, values_split, own_lengths, (fresh_one, fresh_two)
    ).reshape(row_count, -1)
    attended_two = trade(attended_two, leaving, came_from)
    out_two = mix_out(attended_two, w_out)
    return (out_one, out_two)


def solution(mesh):
    placed = (
        P(("rep", "gy"), "gx"),
        P(("rep", "gy"), "gx"),
        P("gx", "gy"),
        P("gy", "gx"),
        P(("rep", "gx"), None, "gy"),
        P(("rep", "gx"), None, "gy"),
        P(None, "gx"),
        P(None, "gx", None),
        P(None, "gx", None),
    )
    return jax.shard_map(
        body,
        mesh=mesh,
        in_specs=placed,
        out_specs=(P(("rep", "gy"), "gx"), P(("rep", "gy"), "gx")),
        check_vma=False,
    )
```

time: 260 us -> 193 us (0.74)
  waiting for transfers between devices: 120 us -> 72.4 us
  blocking collectives: 18.3 us -> 0 us
  local copies, waits for them, and re-layouts: 25.4 us -> 10.4 us
  starting transfers between devices: 8.51 us -> 23.5 us
  matrix products: 51.8 us -> 39.8 us
  other arithmetic: 21.2 us -> 27.1 us
  between operations: 14.4 us -> 19 us
    reduce_scatter x4 -> x0, waiting for transfers between devices: 87.7 us -> none  [the longest x2 62.9 us: project_rows(): lax.psum_scatter(jnp.dot(gathered, w_qkv, preferred_element_type=jnp.floa...]
    ppermute x0 -> x18, waiting for transfers between devices: none -> 72.4 us  [the longest x12 72.4 us: swap(): return lax.ppermute(value, axis, [(i, i ^ bit) for i in range(count)])]
    ppermute x0 -> x18, starting transfers between devices: none -> 23.5 us  [the longest x12 18.5 us: swap(): return lax.ppermute(value, axis, [(i, i ^ bit) for i in range(count)])]
    all_gather x2 -> x0, blocking collectives: 18.3 us -> none  [project_rows(): gathered = lax.all_gather(hidden, 'gy', axis=0, tiled=True)]
    all_gather x2 -> x0, waiting for transfers between devices: 17.3 us -> none  [mix_out(): lax.all_gather(attended, 'gx', axis=0, tiled=True)]
    gather x9 -> x2, local copies, waits for them, and re-layouts: 15.9 us -> 1.3 us  [trade(): own = table[slots]]
    all_to_all x2 -> x0, waiting for transfers between devices: 14.5 us -> none  [the longest x1 14.5 us: body(): lax.all_to_all(spread(send_hit, keys_one[leaving]), 'rep', split_axis=0,...]
    dot_general x8 -> x6, matrix products: 47 us -> 32.9 us  [the longest x2 13.1 us: project_sums(): jnp.dot(jnp.concatenate(blocks, axis=0), w_qkv, preferred_element_type=jn...]
  transfers between devices with their start and end apart: 8 -> 18, of which waited for: 6 -> 9; matrix products, arithmetic and copies ran while one was open for 34% -> 31% of each run, Pallas kernels for 0% -> 0%
where the time goes in v1:
time: 193 us; the launch traced here: 192 us
  waiting for transfers between devices  72.4 us (38%)
  matrix products  39.8 us (21%)
  other arithmetic  27.1 us (14%)
  starting transfers between devices  23.5 us (12%)
  between operations  19 us (10%)
  local copies, waits for them, and re-layouts  10.4 us (5%)
    ppermute x12, waiting for transfers between devices, swap(): return lax.ppermute(value, axis, [(i, i ^ bit) for i in range(count)])  72.4 us
    ppermute x12, starting transfers between devices, swap(): return lax.ppermute(value, axis, [(i, i ^ bit) for i in range(count)])  18.5 us
    dot_general x2, matrix products, project_sums(): jnp.dot(jnp.concatenate(blocks, axis=0), w_qkv, preferred_element_type=jn...  13.1 us
    dot_general x2, matrix products, mix_out(): partial = jnp.dot(lined, w_out, preferred_element_type=jnp.float32)  10.8 us
    dot_general x2, matrix products, cache_part(): jnp.einsum('ngjd,nsgd->ngjs', queries, keys_split, preferred_element_type...  9.1 us
    dot_general x2, matrix products, cache_part(): jnp.einsum('ngjs,nsgd->ngjd', weights.astype(jnp.bfloat16), values_split,...  6.89 us
    ppermute x6, starting transfers between devices, trade(): lax.ppermute(own, 'rep', [(i, (i + m) % count) for i in range(count)])  5.02 us
    eq x4, other arithmetic, trade(): table = jnp.where((row_ids == slots[s])[:, None], got[None], table)  4.87 us
  transfers between devices with their start and end apart: 18, of which 9 were waited for; matrix products, arithmetic and copies ran while one was open for 31% of the time, Pallas kernels for 0%

profile of v1, /device:TPU:0, one launch (start us, length us, event | category | flops | bytes accessed | tf_op | source)
XLA Modules:
  0.0 192.2 jit_solution(15346006904509332948)
XLA Ops:
  0.6 3.0 %collective-permute-start.6 = (bf16[64,2048]{1,0:T(8,128)(2,1)}, bf16[64,2048]{1,0:T(8,128)(2,1)S(1)}, u32[]{:S(2)}, u32[]{:S(2)}) collective-permute-start(bf16[64,2048]{1,0:T(8,128)(2,1)} %param.12), channel_id=1, source_target_pairs={{0,1},{1,0},{2,3},{3,2},{4,5},{5,4},{6,7},{7,6},{8,9},{9,8},{10,11... | collective-permute-start | bytes 786440 | tf_op jit(solution)/shard_map/ppermute | solution.py:20
  4.0 0.8 fusion.120
  5.6 0.9 fusion.121
  7.5 0.9 select_reduce_fusion.2
  9.1 1.2 iota_compare_fusion.4
  10.3 1.2 iota_compare_fusion.5
  11.5 1.3 iota_compare_fusion.6
  14.8 1.2 iota_compare_fusion.7
  31.1 1.5 fusion.140
  35.1 0.8 multiply_cosine_fusion
  35.9 1.0 broadcast_select_fusion
  37.3 8.7 %fusion.77 = f32[128,5120]{1,0:T(8,128)S(1)} fusion(bf16[2048,5120]{1,0:T(8,128)(2,1)} %param.13, bf16[32,2048]{1,0:T(8,128)(2,1)S(1)} %get-tuple-element.43, bf16[32,2048]{1,0:T(8,128)(2,1)S(1)} %get-tuple-element.42, bf16[32,2048]{1,0:T(8,128)(2,1)S(1)} %get-tuple-element.41, bf16[32,2048]{1,0:T(8,128)(2,1)S(1)} %get-tuple-element.40), kind=kOutput, calls=%fused_computation.95 | convolution fusion | flops 2686451712 | bytes 24117248 | tf_op jit(solution)/shard_map/dot_general | solution.py:54
  46.1 2.1 %collective-permute-start.7 = (f16[64,5120]{1,0:T(8,128)(2,1)S(1)}, f16[64,5120]{1,0:T(8,128)(2,1)S(1)}, u32[]{:S(2)}, u32[]{:S(2)}) collective-permute-start(f16[64,5120]{1,0:T(8,128)(2,1)S(1)} %fusion.12), channel_id=1, source_target_pairs={{0,2},{2,0},{4,6},{6,4},{1,3},{3,1},{5,7},{7,5},{8,10},{10,8},{12,... | collective-permute-start | bytes 1966088 | tf_op jit(solution)/shard_map/ppermute | solution.py:20
  48.6 1.7 copy-done
  50.3 4.4 %fusion.69 = f32[128,5120]{1,0:T(8,128)} fusion(bf16[2048,5120]{1,0:T(8,128)(2,1)S(1)} %copy-done, bf16[32,2048]{1,0:T(8,128)(2,1)S(1)} %get-tuple-element.49, bf16[32,2048]{1,0:T(8,128)(2,1)S(1)} %get-tuple-element.48, bf16[32,2048]{1,0:T(8,128)(2,1)S(1)} %get-tuple-element.47, bf16[32,2048]{1,0:T(8,128)(2,1)S(1)} %get-tuple-element.46), kind=kOutput, calls=%fused_computation.84 | convolution fusion | flops 2686451712 | bytes 24117248 | tf_op jit(solution)/shard_map/dot_general | solution.py:54
  54.7 1.6 fusion.13
  56.2 2.1 %collective-permute-start.1 = (f16[64,5120]{1,0:T(8,128)(2,1)S(1)}, f16[64,5120]{1,0:T(8,128)(2,1)S(1)}, u32[]{:S(2)}, u32[]{:S(2)}) collective-permute-start(f16[64,5120]{1,0:T(8,128)(2,1)S(1)} %fusion.13), channel_id=1, source_target_pairs={{0,2},{2,0},{4,6},{6,4},{1,3},{3,1},{5,7},{7,5},{8,10},{10,8},{12,... | collective-permute-start | bytes 1966088 | tf_op jit(solution)/shard_map/ppermute | solution.py:20
  58.3 5.4 %collective-permute-done.7 = f16[64,5120]{1,0:T(8,128)(2,1)S(1)} collective-permute-done((f16[64,5120]{1,0:T(8,128)(2,1)S(1)}, f16[64,5120]{1,0:T(8,128)(2,1)S(1)}, u32[]{:S(2)}, u32[]{:S(2)}) %collective-permute-start.7) | collective-permute-done | bytes 655392 | tf_op jit(solution)/shard_map/ppermute | solution.py:20
  64.0 3.1 %collective-permute-start.8 = (f16[32,5120]{1,0:T(8,128)(2,1)S(1)}, f16[32,5120]{1,0:T(8,128)(2,1)S(1)}, u32[]{:S(2)}, u32[]{:S(2)}) collective-permute-start(f16[32,5120]{1,0:T(8,128)(2,1)S(1)} %fusion.63), channel_id=1, source_target_pairs={{0,4},{2,6},{4,0},{6,2},{1,5},{3,7},{5,1},{7,3},{8,12},{10,14},{12... | collective-permute-start | bytes 983048 | tf_op jit(solution)/shard_map/ppermute | solution.py:20
  67.1 16.3 %collective-permute-done.1 = f16[64,5120]{1,0:T(8,128)(2,1)S(1)} collective-permute-done((f16[64,5120]{1,0:T(8,128)(2,1)S(1)}, f16[64,5120]{1,0:T(8,128)(2,1)S(1)}, u32[]{:S(2)}, u32[]{:S(2)}) %collective-permute-start.1) | collective-permute-done | bytes 655392 | tf_op jit(solution)/shard_map/ppermute | solution.py:20
  83.6 0.8 fusion.64
  84.4 1.8 collective-permute-start.2
  88.3 1.6 collective-permute-start.10
  89.9 1.7 collective-permute-start.9
  91.6 9.3 %collective-permute-done.2 = f16[32,5120]{1,0:T(8,128)(2,1)} collective-permute-done((f16[32,5120]{1,0:T(8,128)(2,1)}, f16[32,5120]{1,0:T(8,128)(2,1)}, u32[]{:S(2)}, u32[]{:S(2)}) %collective-permute-start.2) | collective-permute-done | bytes 327712 | tf_op jit(solution)/shard_map/ppermute | solution.py:20
  100.9 1.9 slice_add_fusion.3
  102.8 1.2 reshape.440
  104.8 1.3 add_convert_fusion.1
  106.1 4.5 %fusion.14 = f32[32,4,8,128]{3,2,1,0:T(8,128)S(1)} fusion(bf16[32,4,9,64]{3,2,1,0:T(8,128)(2,1)S(1)} %get-tuple-element.29, bf16[32,4,9,64]{3,2,1,0:T(8,128)(2,1)S(1)} %get-tuple-element.28, bf16[32,128,512]{2,1,0:T(8,128)(2,1)} %param.15), kind=kOutput, calls=%fused_computation.20 | convolution fusion | flops 34209792 | bytes 5013504 | tf_op jit(solution)/shard_map/ngjd,nsgd->ngjs/dot_general | solution.py:86
  110.8 1.1 fusion.109
  111.9 1.1 fusion.110
  113.1 0.8 select_select_fusion
  114.0 0.8 fusion.65
  115.0 4.6 %select_reduce_fusion = (f32[32,4,8]{2,1,0:T(4,128)S(1)}, f32[32,4,8]{2,1,0:T(4,128)S(1)}, f32[32,4,8,128]{3,2,1,0:T(8,128)S(1)}) fusion(pred[32,128]{1,0:T(8,128)(4,1)} %iota_compare_fusion, f32[32,4,8,128]{3,2,1,0:T(8,128)S(1)} %fusion.14, bf16[32,4,10,128]{3,2,1,0:T(8,128)(2,1)S(1)} %select_select_fusion, bf16[32,128,512]{2,1,0:T(8,128)(2,1)} %param.15), kind=kOutput, calls=%fused_computation.106 | convolution fusion | flops 34207744 | bytes 5517312 | tf_op jit(solution)/shard_map/ngjd,nsgd->ngjs/dot_general | solution.py:86
  120.9 3.4 %fusion.44 = bf16[32,4,8,128]{3,2,1,0:T(8,128)(2,1)S(1)} fusion(f32[32,4,8,128]{3,2,1,0:T(8,128)S(1)} %get-tuple-element.74, f32[32,4,8]{2,1,0:T(4,128)S(1)} %copy.62, f32[32,4,128]{2,1,0:T(4,128)S(1)} %bitcast.124, f32[32,4,8]{2,1,0:T(4,128)S(1)} %copy.60, f32[32,4,8]{2,1,0:T(4,128)S(1)} %copy.59, f32[32,4,8]{2,1,0:T(4,128)S(1)} %get-tuple-element.15, ...), kind=kOutput, calls=%fused_computation.30 | convolution fusion | flops 34865152 | bytes 5136384 | tf_op jit(solution)/shard_map/ngjs,nsgd->ngjd/dot_general | solution.py:91
  125.3 1.4 collective-permute-start.13
  127.5 3.4 %fusion.38 = bf16[32,4,8,128]{3,2,1,0:T(8,128)(2,1)S(1)} fusion(f32[32,4,8,128]{3,2,1,0:T(8,128)S(1)} %fusion.14, f32[32,4,8]{2,1,0:T(4,128)S(1)} %copy.50, f32[32,4,128]{2,1,0:T(4,128)S(1)} %bitcast.123, f32[32,4,8]{2,1,0:T(4,128)S(1)} %copy.48, f32[32,4,8]{2,1,0:T(4,128)S(1)} %get-tuple-element.16, f32[32,4,8]{2,1,0:T(4,128)S(1)} %copy.46, ...), kind=kOutput, calls=%fused_computation.28 | convolution fusion | flops 34603008 | bytes 5066752 | tf_op jit(solution)/shard_map/ngjs,nsgd->ngjd/dot_general | solution.py:91
  131.8 3.0 %collective-permute-start.15 = (bf16[32,4096]{1,0:T(8,128)(2,1)S(1)}, bf16[32,4096]{1,0:T(8,128)(2,1)S(1)}, u32[]{:S(2)}, u32[]{:S(2)}) collective-permute-start(bf16[32,4096]{1,0:T(8,128)(2,1)S(1)} %select_select_fusion.1), channel_id=1, source_target_pairs={{0,4},{2,6},{4,0},{6,2},{1,5},{3,7},{5,1},{7,3},{8,12},{10,14},{12... | collective-permute-start | bytes 786440 | tf_op jit(solution)/shard_map/ppermute | solution.py:20
  134.8 17.5 %collective-permute-done.3 = bf16[32,4096]{1,0:T(8,128)(2,1)S(1)} collective-permute-done((bf16[32,4096]{1,0:T(8,128)(2,1)S(1)}, bf16[32,4096]{1,0:T(8,128)(2,1)S(1)}, u32[]{:S(2)}, u32[]{:S(2)}) %collective-permute-start.3) | collective-permute-done | bytes 262176 | tf_op jit(solution)/shard_map/ppermute | solution.py:20
  152.4 5.4 %collective-permute-done.15 = bf16[32,4096]{1,0:T(8,128)(2,1)S(1)} collective-permute-done((bf16[32,4096]{1,0:T(8,128)(2,1)S(1)}, bf16[32,4096]{1,0:T(8,128)(2,1)S(1)}, u32[]{:S(2)}, u32[]{:S(2)}) %collective-permute-start.15) | collective-permute-done | bytes 262176 | tf_op jit(solution)/shard_map/ppermute | solution.py:20
  158.0 11.1 %collective-permute-done.4 = bf16[64,4096]{1,0:T(8,128)(2,1)S(1)} collective-permute-done((bf16[64,4096]{1,0:T(8,128)(2,1)S(1)}, bf16[64,4096]{1,0:T(8,128)(2,1)S(1)}, u32[]{:S(2)}, u32[]{:S(2)}) %collective-permute-start.4) | collective-permute-done | bytes 524320 | tf_op jit(solution)/shard_map/ppermute | solution.py:20
  169.3 8.3 %fusion.47 = f32[128,2048]{1,0:T(8,128)S(1)} fusion(bf16[4096,2048]{1,0:T(8,128)(2,1)} %param.14, bf16[32,4096]{1,0:T(8,128)(2,1)S(1)} %get-tuple-element.35, bf16[32,4096]{1,0:T(8,128)(2,1)S(1)} %get-tuple-element.36, bf16[32,4096]{1,0:T(8,128)(2,1)S(1)} %get-tuple-element.37, bf16[32,4096]{1,0:T(8,128)(2,1)S(1)} %get-tuple-element.34), kind=kOutput, calls=%fused_computation.31 | convolution fusion | flops 2151677952 | bytes 18874368 | tf_op jit(solution)/shard_map/dot_general | solution.py:146
  177.6 1.5 collective-permute-start.5
  179.2 1.1 collective-permute-done.16
  180.4 2.4 %fusion.55 = f32[128,2048]{1,0:T(8,128)S(1)} fusion(bf16[4096,2048]{1,0:T(8,128)(2,1)S(1)} %bitcast.129, bf16[32,4096]{1,0:T(8,128)(2,1)S(1)} %get-tuple-element.31, bf16[32,4096]{1,0:T(8,128)(2,1)S(1)} %get-tuple-element.32, bf16[32,4096]{1,0:T(8,128)(2,1)S(1)} %get-tuple-element.33, bf16[32,4096]{1,0:T(8,128)(2,1)S(1)} %get-tuple-element.30), kind=kOutput, calls=%fused_computation.40 | convolution fusion | flops 2151677952 | bytes 18874368 | tf_op jit(solution)/shard_map/dot_general | solution.py:146
  182.9 1.5 collective-permute-start.17
  184.4 1.6 collective-permute-done.5
  186.8 4.6 %collective-permute-done.17 = bf16[64,2048]{1,0:T(8,128)(2,1)S(1)} collective-permute-done((bf16[64,2048]{1,0:T(8,128)(2,1)S(1)}, bf16[64,2048]{1,0:T(8,128)(2,1)S(1)}, u32[]{:S(2)}, u32[]{:S(2)}) %collective-permute-start.17) | collective-permute-done | bytes 262176 | tf_op jit(solution)/shard_map/ppermute | solution.py:20
  (130 shorter events, 15.1 us)
Async XLA Ops:
  0.6 35.3 %collective-permute-start.6 = (bf16[64,2048]{1,0:T(8,128)(2,1)}, bf16[64,2048]{1,0:T(8,128)(2,1)S(1)}, u32[]{:S(2)}, u32[]{:S(2)}) collective-permute-start(bf16[64,2048]{1,0:T(8,128)(2,1)} %param.12), channel_id=1, source_target_pairs={{0,1},{1,0},{2,3},{3,2},{4,5},{5,4},{6,7},{7,6},{8,9},{9,8},{10,11... | collective-permute-start | bytes 786440 | tf_op jit(solution)/shard_map/ppermute | solution.py:20
  3.7 44.5 %collective-permute-start = (bf16[64,2048]{1,0:T(8,128)(2,1)}, bf16[64,2048]{1,0:T(8,128)(2,1)S(1)}, u32[]{:S(2)}, u32[]{:S(2)}) collective-permute-start(bf16[64,2048]{1,0:T(8,128)(2,1)} %param.11), channel_id=1, source_target_pairs={{0,1},{1,0},{2,3},{3,2},{4,5},{5,4},{6,7},{7,6},{8,9},{9,8},{10,11... | collective-permute-start | bytes 786440 | tf_op jit(solution)/shard_map/ppermute | solution.py:20
  8.4 79.3 %copy-start.5 = (s32[1024]{0:T(1024)}, s32[1024]{0:T(1024)S(1)}, u32[]{:S(2)}) copy-start(s32[1024]{0:T(1024)S(1)} %pad_clamp_fusion) | copy-start | bytes 12292
  37.2 10.9 %copy-start.2 = (bf16[64,2048]{1,0:T(8,128)(2,1)S(1)}, bf16[64,2048]{1,0:T(8,128)(2,1)}, u32[]{:S(2)}) copy-start(bf16[64,2048]{1,0:T(8,128)(2,1)} %param.11) | copy-start | bytes 786436
  37.3 13.0 %copy-start = (bf16[2048,5120]{1,0:T(8,128)(2,1)S(1)}, bf16[2048,5120]{1,0:T(8,128)(2,1)}, u32[]{:S(2)}) copy-start(bf16[2048,5120]{1,0:T(8,128)(2,1)} %param.13) | copy-start | bytes 62914564
  46.1 17.7 %collective-permute-start.7 = (f16[64,5120]{1,0:T(8,128)(2,1)S(1)}, f16[64,5120]{1,0:T(8,128)(2,1)S(1)}, u32[]{:S(2)}, u32[]{:S(2)}) collective-permute-start(f16[64,5120]{1,0:T(8,128)(2,1)S(1)} %fusion.12), channel_id=1, source_target_pairs={{0,2},{2,0},{4,6},{6,4},{1,3},{3,1},{5,7},{7,5},{8,10},{10,8},{12,... | collective-permute-start | bytes 1966088 | tf_op jit(solution)/shard_map/ppermute | solution.py:20
  54.7 28.7 %copy-start.1 = (f32[128,5120]{1,0:T(8,128)S(1)}, f32[128,5120]{1,0:T(8,128)}, u32[]{:S(2)}) copy-start(f32[128,5120]{1,0:T(8,128)} %fusion.69) | copy-start | bytes 7864324
  56.2 27.2 %collective-permute-start.1 = (f16[64,5120]{1,0:T(8,128)(2,1)S(1)}, f16[64,5120]{1,0:T(8,128)(2,1)S(1)}, u32[]{:S(2)}, u32[]{:S(2)}) collective-permute-start(f16[64,5120]{1,0:T(8,128)(2,1)S(1)} %fusion.13), channel_id=1, source_target_pairs={{0,2},{2,0},{4,6},{6,4},{1,3},{3,1},{5,7},{7,5},{8,10},{10,8},{12,... | collective-permute-start | bytes 1966088 | tf_op jit(solution)/shard_map/ppermute | solution.py:20
  64.0 22.3 %collective-permute-start.8 = (f16[32,5120]{1,0:T(8,128)(2,1)S(1)}, f16[32,5120]{1,0:T(8,128)(2,1)S(1)}, u32[]{:S(2)}, u32[]{:S(2)}) collective-permute-start(f16[32,5120]{1,0:T(8,128)(2,1)S(1)} %fusion.63), channel_id=1, source_target_pairs={{0,4},{2,6},{4,0},{6,2},{1,5},{3,7},{5,1},{7,3},{8,12},{10,14},{12... | collective-permute-start | bytes 983048 | tf_op jit(solution)/shard_map/ppermute | solution.py:20
  84.4 16.6 %collective-permute-start.2 = (f16[32,5120]{1,0:T(8,128)(2,1)}, f16[32,5120]{1,0:T(8,128)(2,1)}, u32[]{:S(2)}, u32[]{:S(2)}) collective-permute-start(f16[32,5120]{1,0:T(8,128)(2,1)} %fusion.64), channel_id=1, source_target_pairs={{0,4},{2,6},{4,0},{6,2},{1,5},{3,7},{5,1},{7,3},{8,12},{10,14},{12... | collective-permute-start | bytes 983048 | tf_op jit(solution)/shard_map/ppermute | solution.py:20
  88.3 22.4 %collective-permute-start.10 = (bf16[4,5120]{1,0:T(4,128)(2,1)S(1)}, bf16[4,5120]{1,0:T(4,128)(2,1)S(1)}, u32[]{:S(2)}, u32[]{:S(2)}) collective-permute-start(bf16[4,5120]{1,0:T(4,128)(2,1)S(1)} %gather_fusion), channel_id=1, source_target_pairs={{0,16},{8,24},{16,0},{24,8},{1,17},{9,25},{17,1},{25,9},{2,18},{10... | collective-permute-start | bytes 122888 | tf_op jit(solution)/shard_map/ppermute | solution.py:157
  89.9 20.9 %collective-permute-start.11 = (bf16[4,5120]{1,0:T(4,128)(2,1)S(1)}, bf16[4,5120]{1,0:T(4,128)(2,1)}, u32[]{:S(2)}, u32[]{:S(2)}) collective-permute-start(bf16[4,5120]{1,0:T(4,128)(2,1)S(1)} %gather_fusion), channel_id=1, source_target_pairs={{0,8},{8,16},{16,24},{24,0},{1,9},{9,17},{17,25},{25,1},{2,10},{10... | collective-permute-start | bytes 122888 | tf_op jit(solution)/shard_map/ppermute | solution.py:157
  89.9 20.9 %collective-permute-start.9 = (bf16[4,5120]{1,0:T(4,128)(2,1)S(1)}, bf16[4,5120]{1,0:T(4,128)(2,1)}, u32[]{:S(2)}, u32[]{:S(2)}) collective-permute-start(bf16[4,5120]{1,0:T(4,128)(2,1)S(1)} %gather_fusion), channel_id=1, source_target_pairs={{0,24},{8,0},{16,8},{24,16},{1,25},{9,1},{17,9},{25,17},{2,26},{10... | collective-permute-start | bytes 122888 | tf_op jit(solution)/shard_map/ppermute | solution.py:157
  106.0 7.0 %copy-start.6 = (pred[32]{0:T(512)(128)(4,1)S(1)}, pred[32]{0:T(512)(128)(4,1)}, u32[]{:S(2)}) copy-start(pred[32]{0:T(512)(128)(4,1)} %iota_compare_fusion.4) | copy-start | bytes 100
  106.0 7.0 %copy-start.8 = (pred[32]{0:T(512)(128)(4,1)S(1)}, pred[32]{0:T(512)(128)(4,1)}, u32[]{:S(2)}) copy-start(pred[32]{0:T(512)(128)(4,1)} %iota_compare_fusion.5) | copy-start | bytes 100
  106.0 7.0 %copy-start.10 = (pred[32]{0:T(512)(128)(4,1)S(1)}, pred[32]{0:T(512)(128)(4,1)}, u32[]{:S(2)}) copy-start(pred[32]{0:T(512)(128)(4,1)} %iota_compare_fusion.6) | copy-start | bytes 100
  106.1 7.0 %copy-start.12 = (pred[32]{0:T(512)(128)(4,1)S(1)}, pred[32]{0:T(512)(128)(4,1)}, u32[]{:S(2)}) copy-start(pred[32]{0:T(512)(128)(4,1)} %iota_compare_fusion.7) | copy-start | bytes 100
  115.0 4.7 %copy-start.4 = (pred[32,128]{1,0:T(8,128)(4,1)S(1)}, pred[32,128]{1,0:T(8,128)(4,1)}, u32[]{:S(2)}) copy-start(pred[32,128]{1,0:T(8,128)(4,1)} %iota_compare_fusion) | copy-start | bytes 12292
  115.0 6.0 %copy-start.3 = (f32[32,4,1,128]{3,2,1,0:T(1,128)S(1)}, f32[32,4,1,128]{3,2,1,0:T(1,128)}, u32[]{:S(2)}) copy-start(f32[32,4,1,128]{3,2,1,0:T(1,128)} %fusion.107) | copy-start | bytes 196612
  125.2 6.0 %collective-permute-start.12 = (bf16[4,4096]{1,0:T(4,128)(2,1)S(1)}, bf16[4,4096]{1,0:T(4,128)(2,1)S(1)}, u32[]{:S(2)}, u32[]{:S(2)}) collective-permute-start(bf16[4,4096]{1,0:T(4,128)(2,1)S(1)} %gather_fusion.1), channel_id=1, source_target_pairs={{0,24},{8,0},{16,8},{24,16},{1,25},{9,1},{17,9},{25,17},{2,26},{10... | collective-permute-start | bytes 98312 | tf_op jit(solution)/shard_map/ppermute | solution.py:157
  125.3 5.9 %collective-permute-start.13 = (bf16[4,4096]{1,0:T(4,128)(2,1)S(1)}, bf16[4,4096]{1,0:T(4,128)(2,1)S(1)}, u32[]{:S(2)}, u32[]{:S(2)}) collective-permute-start(bf16[4,4096]{1,0:T(4,128)(2,1)S(1)} %gather_fusion.1), channel_id=1, source_target_pairs={{0,16},{8,24},{16,0},{24,8},{1,17},{9,25},{17,1},{25,9},{2,18},{10... | collective-permute-start | bytes 98312 | tf_op jit(solution)/shard_map/ppermute | solution.py:157
  126.7 4.5 %collective-permute-start.14 = (bf16[4,4096]{1,0:T(4,128)(2,1)S(1)}, bf16[4,4096]{1,0:T(4,128)(2,1)S(1)}, u32[]{:S(2)}, u32[]{:S(2)}) collective-permute-start(bf16[4,4096]{1,0:T(4,128)(2,1)S(1)} %gather_fusion.1), channel_id=1, source_target_pairs={{0,8},{8,16},{16,24},{24,0},{1,9},{9,17},{17,25},{25,1},{2,10},{10... | collective-permute-start | bytes 98312 | tf_op jit(solution)/shard_map/ppermute | solution.py:157
  127.4 4.2 %copy-start.7 = (pred[32]{0:T(512)(128)(4,1)S(1)}, pred[32]{0:T(512)(128)(4,1)}, u32[]{:S(2)}) copy-start(pred[32]{0:T(512)(128)(4,1)} %iota_compare_fusion.4) | copy-start | bytes 100
  127.4 4.2 %copy-start.9 = (pred[32]{0:T(512)(128)(4,1)S(1)}, pred[32]{0:T(512)(128)(4,1)}, u32[]{:S(2)}) copy-start(pred[32]{0:T(512)(128)(4,1)} %iota_compare_fusion.5) | copy-start | bytes 100
  127.4 4.2 %copy-start.11 = (pred[32]{0:T(512)(128)(4,1)S(1)}, pred[32]{0:T(512)(128)(4,1)}, u32[]{:S(2)}) copy-start(pred[32]{0:T(512)(128)(4,1)} %iota_compare_fusion.6) | copy-start | bytes 100
  127.5 4.2 %copy-start.13 = (pred[32]{0:T(512)(128)(4,1)S(1)}, pred[32]{0:T(512)(128)(4,1)}, u32[]{:S(2)}) copy-start(pred[32]{0:T(512)(128)(4,1)} %iota_compare_fusion.7) | copy-start | bytes 100
  131.1 21.1 %collective-permute-start.3 = (bf16[32,4096]{1,0:T(8,128)(2,1)S(1)}, bf16[32,4096]{1,0:T(8,128)(2,1)S(1)}, u32[]{:S(2)}, u32[]{:S(2)}) collective-permute-start(bf16[32,4096]{1,0:T(8,128)(2,1)S(1)} %bitcast.118), channel_id=1, source_target_pairs={{0,4},{2,6},{4,0},{6,2},{1,5},{3,7},{5,1},{7,3},{8,12},{10,14},{12... | collective-permute-start | bytes 786440 | tf_op jit(solution)/shard_map/ppermute | solution.py:20
  131.8 26.0 %collective-permute-start.15 = (bf16[32,4096]{1,0:T(8,128)(2,1)S(1)}, bf16[32,4096]{1,0:T(8,128)(2,1)S(1)}, u32[]{:S(2)}, u32[]{:S(2)}) collective-permute-start(bf16[32,4096]{1,0:T(8,128)(2,1)S(1)} %select_select_fusion.1), channel_id=1, source_target_pairs={{0,4},{2,6},{4,0},{6,2},{1,5},{3,7},{5,1},{7,3},{8,12},{10,14},{12... | collective-permute-start | bytes 786440 | tf_op jit(solution)/shard_map/ppermute | solution.py:20
  152.3 16.8 %collective-permute-start.4 = (bf16[64,4096]{1,0:T(8,128)(2,1)S(1)}, bf16[64,4096]{1,0:T(8,128)(2,1)S(1)}, u32[]{:S(2)}, u32[]{:S(2)}) collective-permute-start(bf16[64,4096]{1,0:T(8,128)(2,1)S(1)} %pad_maximum_fusion.1), channel_id=1, source_target_pairs={{0,2},{2,0},{4,6},{6,4},{1,3},{3,1},{5,7},{7,5},{8,10},{10,8},{12,... | collective-permute-start | bytes 1572872 | tf_op jit(solution)/shard_map/ppermute | solution.py:20
  157.9 22.3 %collective-permute-start.16 = (bf16[64,4096]{1,0:T(8,128)(2,1)S(1)}, bf16[64,4096]{1,0:T(8,128)(2,1)S(1)}, u32[]{:S(2)}, u32[]{:S(2)}) collective-permute-start(bf16[64,4096]{1,0:T(8,128)(2,1)S(1)} %pad_maximum_fusion.3), channel_id=1, source_target_pairs={{0,2},{2,0},{4,6},{6,4},{1,3},{3,1},{5,7},{7,5},{8,10},{10,8},{12,... | collective-permute-start | bytes 1572872 | tf_op jit(solution)/shard_map/ppermute | solution.py:20
  169.2 11.2 %slice-start = ((s8[16777216]{0:T(1024)(128)(4,1)}), s8[4194304]{0:T(1024)(128)(4,1)S(1)}, s32[]{:S(2)}) async-start(s8[16777216]{0:T(1024)(128)(4,1)} %bitcast.128), calls=%async_computation | async-start | bytes 8388608
  169.2 11.2 %slice-start.1 = ((s8[16777216]{0:T(1024)(128)(4,1)}), s8[4194304]{0:T(1024)(128)(4,1)S(1)}, s32[]{:S(2)}) async-start(s8[16777216]{0:T(1024)(128)(4,1)} %bitcast.128), calls=%async_computation.1 | async-start | bytes 8388608
  169.2 11.2 %slice-start.2 = ((s8[16777216]{0:T(1024)(128)(4,1)}), s8[4194304]{0:T(1024)(128)(4,1)S(1)}, s32[]{:S(2)}) async-start(s8[16777216]{0:T(1024)(128)(4,1)} %bitcast.128), calls=%async_computation.2 | async-start | bytes 8388608
  169.2 11.2 %slice-start.3 = ((s8[16777216]{0:T(1024)(128)(4,1)}), s8[4194304]{0:T(1024)(128)(4,1)S(1)}, s32[]{:S(2)}) async-start(s8[16777216]{0:T(1024)(128)(4,1)} %bitcast.128), calls=%async_computation.3 | async-start | bytes 8388608
  177.6 8.4 %collective-permute-start.5 = (bf16[64,2048]{1,0:T(8,128)(2,1)S(1)}, bf16[64,2048]{1,0:T(8,128)(2,1)S(1)}, u32[]{:S(2)}, u32[]{:S(2)}) collective-permute-start(bf16[64,2048]{1,0:T(8,128)(2,1)S(1)} %slice.444), channel_id=1, source_target_pairs={{0,1},{1,0},{2,3},{3,2},{4,5},{5,4},{6,7},{7,6},{8,9},{9,8},{10,11... | collective-permute-start | bytes 786440 | tf_op jit(solution)/shard_map/ppermute | solution.py:20
  182.9 8.5 %collective-permute-start.17 = (bf16[64,2048]{1,0:T(8,128)(2,1)S(1)}, bf16[64,2048]{1,0:T(8,128)(2,1)S(1)}, u32[]{:S(2)}, u32[]{:S(2)}) collective-permute-start(bf16[64,2048]{1,0:T(8,128)(2,1)S(1)} %slice.443), channel_id=1, source_target_pairs={{0,1},{1,0},{2,3},{3,2},{4,5},{5,4},{6,7},{7,6},{8,9},{9,8},{10,11... | collective-permute-start | bytes 786440 | tf_op jit(solution)/shard_map/ppermute | solution.py:20

commit v2 on v1

v2 whole, which is shorter than its diff:
```python
import math

import jax
import jax.numpy as jnp
from jax import lax
from jax.experimental import pallas as pl
from jax.experimental.pallas import tpu as pltpu
from jax.sharding import PartitionSpec as P


HEADS = 64
KV_HEADS = 8
HEAD_DIM = 128
ROWS_DEV = 16
GROUP = HEADS // KV_HEADS
ROPE_BASE = 500000.0
LINK_SCALE = 16.0
STEP = 16
CHUNKS = 2
SCORE_SCALE = 1.0 / math.sqrt(HEAD_DIM)


def swap(value, axis, bit):
    count = lax.axis_size(axis)
    return lax.ppermute(value, axis, [(i, i ^ bit) for i in range(count)])


def power_of_two(count):
    return count & (count - 1) == 0


def gather_rows(hidden, after=None):
    if lax.axis_size("gy") != 2:
        return lax.all_gather(hidden, "gy", axis=0, tiled=True)
    peer = swap(hidden, "gy", 1)
    if after is not None:
        peer, _ = lax.optimization_barrier((peer, after))
    first = lax.axis_index("gy") == 0
    return jnp.concatenate([jnp.where(first, hidden, peer), jnp.where(first, peer, hidden)], axis=0)


def narrow(value):
    return (value * LINK_SCALE).astype(jnp.float16)


def widen(value):
    return value.astype(jnp.float32) * (1.0 / LINK_SCALE)


def line_up(gathered):
    count = lax.axis_size("gx")
    if not power_of_two(count):
        return gathered
    place = lax.axis_index("gx")
    rows = gathered.shape[0] // count
    order = sorted(range(count), key=lambda k: [1 - (k >> b & 1) for b in range(count.bit_length() - 1)])
    blocks = [lax.dynamic_slice_in_dim(gathered, (place ^ k) * rows, rows, 0) for k in order]
    return jnp.concatenate(blocks, axis=0)


def project_sums(lined, w_qkv, chunks, after=None):
    count = lax.axis_size("gx")
    width = w_qkv.shape[1] // chunks
    parts = []
    for c in range(chunks):
        weights = w_qkv[:, c * width : (c + 1) * width]
        parts.append(jnp.dot(lined, weights, preferred_element_type=jnp.float32))
    if not power_of_two(count):
        parts = [lax.psum_scatter(part, "gx", scatter_dimension=0, tiled=True) for part in parts]
    sent = parts[0][:1, :1]
    bit = 1
    while bit < count and power_of_two(count):
        half = parts[0].shape[0] // 2
        for c in range(chunks):
            sent = narrow(parts[c][:half])
            received = swap(sent, "gx", bit)
            if after is not None:
                received, _ = lax.optimization_barrier((received, after))
            parts[c] = parts[c][half:] + widen(received)
        bit *= 2
    return parts, sent


def turn_tables(positions):
    half_dim = HEAD_DIM // 2
    inverse = ROPE_BASE ** (-(jnp.arange(half_dim, dtype=jnp.float32) * 2.0 / HEAD_DIM))
    angles = positions.astype(jnp.float32)[:, None] * inverse
    cosine, sine = jnp.cos(angles), jnp.sin(angles)
    return jnp.concatenate([cosine, cosine], axis=-1), jnp.concatenate([-sine, sine], axis=-1)


def attend_block(lengths, sums, cosine, sine, *rest):
    *earlier, keys, values, attended, fresh, turned, merged = rest
    groups = keys.shape[2] // HEAD_DIM
    heads = groups * GROUP
    each = GROUP + 2
    steps = sums.shape[0]
    first = pl.program_id(0) * steps
    slot_ids = lax.broadcasted_iota(jnp.int32, (heads, keys.shape[1]), 1)
    head_group = lax.broadcasted_iota(jnp.int32, (heads, HEAD_DIM), 0) // GROUP

    def lanes(at):
        return slice(at * HEAD_DIM, (at + 1) * HEAD_DIM)

    def stack(per_row):
        return jnp.concatenate([per_row(r) for r in range(steps)], axis=0)

    def over_heads(table, base):
        return stack(
            lambda r: jnp.concatenate(
                [jnp.broadcast_to(table[r : r + 1, lanes(2 * g + base)], (GROUP, HEAD_DIM)) for g in range(groups)],
                axis=0,
            )
        )

    for at in range(groups * each):
        block = sums[:, lanes(at)]
        if at % each <= GROUP:
            block = block * cosine[...] + pltpu.roll(block, HEAD_DIM // 2, 1) * sine[...]
        block = block.astype(jnp.bfloat16).astype(jnp.float32)
        if at % each < GROUP:
            turned[pl.ds(at // each * GROUP + at % each, steps, stride=heads), :] = block
        else:
            fresh[:, lanes(at // each * 2 + at % each - GROUP)] = block
    query = turned[...]

    def row_scores(r):
        mine = query[r * heads : (r + 1) * heads]
        spread = jnp.concatenate([jnp.where(head_group == g, mine, 0.0) for g in range(groups)], axis=1)
        raw = lax.dot_general(
            spread.astype(jnp.bfloat16), keys[r], (((1,), (1,)), ((), ())), preferred_element_type=jnp.float32
        )
        return jnp.where(slot_ids < lengths[first + r], raw * SCORE_SCALE, -jnp.inf)

    def row_blend(r):
        whole = jnp.dot(
            weights[r * heads : (r + 1) * heads].astype(jnp.bfloat16), values[r],
            preferred_element_type=jnp.float32,
        )
        return jnp.concatenate(
            [whole[g * GROUP : (g + 1) * GROUP, g * HEAD_DIM : (g + 1) * HEAD_DIM] for g in range(groups)], axis=0
        )

    scores = stack(row_scores)
    highest = jnp.max(scores, axis=1, keepdims=True)
    weights = jnp.exp(scores - highest)
    weight_sum = jnp.sum(weights, axis=1, keepdims=True)
    blended = stack(row_blend)
    sources = list(earlier) + [fresh]
    marks = [
        jnp.sum(query * over_heads(e, 0), axis=1, keepdims=True) * SCORE_SCALE for e in sources
    ]
    joint = highest
    for mark in marks:
        joint = jnp.maximum(joint, mark)
    share = jnp.exp(highest - joint)
    top, bottom = share * blended, share * weight_sum
    for mark, e in zip(marks, sources):
        share = jnp.exp(mark - joint)
        top = top + share * over_heads(e, 1)
        bottom = bottom + share
    merged[...] = top / bottom
    for h in range(heads):
        attended[:, lanes(h)] = merged[pl.ds(h, steps, stride=heads), :].astype(jnp.bfloat16)


def attend(sums, tables, earlier, key_cache, value_cache, lengths, chunk, chunks):
    row_count, slots, width = key_cache.shape
    width = width // chunks
    groups = width // HEAD_DIM
    step = next(n for n in (STEP, 8, 1) if row_count % n == 0)

    def rows(*shape):
        return pl.BlockSpec((step,) + shape, lambda i, _: (i,) + (0,) * len(shape))

    heads = groups * GROUP
    fresh = rows(2 * width)
    before = pl.BlockSpec((step, 2 * width), lambda i, _: (i, chunk))
    cache = pl.BlockSpec((step, slots, width), lambda i, _: (i, 0, chunk))
    return pl.pallas_call(
        attend_block,
        grid_spec=pltpu.PrefetchScalarGridSpec(
            num_scalar_prefetch=1,
            grid=(row_count // step,),
            in_specs=[rows(sums.shape[1]), rows(HEAD_DIM), rows(HEAD_DIM)]
            + [before for _ in earlier]
            + [cache, cache],
            out_specs=[rows(heads * HEAD_DIM), fresh],
            scratch_shapes=[pltpu.VMEM((step * heads, HEAD_DIM), jnp.float32) for _ in range(2)],
        ),
        out_shape=[
            jax.ShapeDtypeStruct((row_count, heads * HEAD_DIM), jnp.bfloat16),
            jax.ShapeDtypeStruct((row_count, 2 * width), jnp.float32),
        ],
        compiler_params=pltpu.CompilerParams(vmem_limit_bytes=16 * 1024 * 1024),
        cost_estimate=pl.CostEstimate(
            flops=8 * row_count * heads * slots * width,
            bytes_accessed=4 * row_count * slots * width,
            transcendentals=0,
        ),
    )(lengths, sums, *tables, *earlier, key_cache, value_cache)


def reverse_bits(value, count):
    turned = value * 0
    bit = count // 2
    while bit:
        turned = turned + (value & 1) * bit
        value = value >> 1
        bit //= 2
    return turned


def spread_rows(own, extra=None):
    held = own
    bit = lax.axis_size("gx") // 2
    while bit:
        sent = held if extra is None or bit > 1 else jnp.concatenate([held, extra], axis=0)
        other = swap(sent, "gx", bit)
        if extra is not None and bit == 1:
            extra = jnp.concatenate([extra, other[held.shape[0] :]], axis=0)
            other = other[: held.shape[0]]
        held = jnp.concatenate([held, other], axis=0)
        bit //= 2
    return held if extra is None else (held, extra)


def by_side(held, rows):
    count = lax.axis_size("gx")
    place, side = lax.axis_index("gx"), lax.axis_index("gy")
    share = count // 2
    spots = [(1 - side) * share + j for j in range(share)] + [side * share + j for j in range(share)]
    return jnp.concatenate(
        [lax.dynamic_slice_in_dim(held, reverse_bits(c ^ place, count) * rows, rows, 0) for c in spots], axis=0
    )


def pairwise():
    count = lax.axis_size("gx")
    return power_of_two(count) and count > 1 and lax.axis_size("gy") == 2


def mix_rows(attended, w_out):
    partial = jnp.dot(
        lax.all_gather(attended, "gx", axis=0, tiled=True), w_out, preferred_element_type=jnp.float32
    )
    return lax.psum_scatter(partial.astype(jnp.bfloat16), "gy", scatter_dimension=0, tiled=True)


def mix_lined(lined, w_out):
    partial, start = None, 0
    for part in lined:
        weights = w_out[start : start + part.shape[1]]
        piece = jnp.dot(part, weights, preferred_element_type=jnp.float32)
        partial = piece if partial is None else partial + piece
        start += part.shape[1]
    half = partial.shape[0] // 2
    received = swap(partial[:half].astype(jnp.bfloat16), "gy", 1)
    return (partial[half:] + received.astype(jnp.float32)).astype(jnp.bfloat16)


def pick_rows(hits, rows):
    return jnp.dot(hits.astype(jnp.bfloat16), rows, preferred_element_type=jnp.float32).astype(jnp.bfloat16)


def all_replicas(own):
    count = lax.axis_size("rep")
    held = [own]
    for m in range(1, count):
        held.append(lax.ppermute(own, "rep", [(i, (i + m) % count) for i in range(count)]))
    return jnp.concatenate(held, axis=0)


def partner_hits(partners):
    count = lax.axis_size("rep")
    slots = partners.shape[0]
    away = jnp.mod(lax.axis_index("rep") - partners, count)
    columns = jnp.arange(count * slots, dtype=jnp.int32)
    return (away * slots + jnp.arange(slots, dtype=jnp.int32))[:, None] == columns[None, :]


def row_hits(row_count, slots):
    return jnp.arange(row_count, dtype=jnp.int32)[:, None] == slots[None, :]


def replace_rows(table, hits, rows):
    return jnp.where(jnp.any(hits, axis=1)[:, None], pick_rows(hits, rows), table)


def table_of_all(local):
    count = lax.axis_size("gx")
    if not power_of_two(count):
        return lax.all_gather(local, "gx", axis=2, tiled=True)
    here = (jnp.arange(count, dtype=jnp.int32) == lax.axis_index("gx"))[None, None, :, None, None]
    full = jnp.where(here, local[:, :, None], 0)
    bit = 1
    while bit < count:
        other = swap(full, "gx", bit)
        full = full + other
        bit *= 2
    return full.reshape(local.shape[0], local.shape[1], -1, local.shape[3])


def own_slots(mig, dest):
    replica = lax.axis_index("rep")
    base = (jnp.arange(mig.shape[1], dtype=jnp.int32) * ROWS_DEV)[:, None]
    leaving = (base + mig[replica]).reshape(-1)
    heading = dest[replica].reshape(-1)
    ids = jnp.arange(mig.shape[0], dtype=jnp.int32)[:, None, None]
    came_from = jnp.sum(jnp.where(dest == replica, ids, 0), axis=0).reshape(-1)
    return leaving, heading, came_from


def steps(hidden_one, hidden_two, w_qkv, w_out, key_cache, value_cache, lengths, mig_rows, dest):
    replica = lax.axis_index("rep")
    own_lengths = lengths[replica]
    row_count = own_lengths.shape[0]
    tables = table_of_all(jnp.stack([mig_rows, dest]))
    side_blocks = tables.shape[2] // lax.axis_size("gy")
    ours = lax.dynamic_slice_in_dim(tables, lax.axis_index("gy") * side_blocks, side_blocks, 2)

    all_leaving, _, _ = own_slots(tables[0], tables[1])

    lined_one = line_up(gather_rows(hidden_one))
    gathered_two = gather_rows(hidden_two, lined_one)
    side_leaving, side_heading, _ = own_slots(ours[0], ours[1])
    side_hits = row_hits(hidden_two.shape[0], side_leaving)
    moved = pick_rows(partner_hits(side_heading), all_replicas(pick_rows(side_hits.T, hidden_two)))
    moved = gather_rows(moved, lined_one)
    gathered_two = replace_rows(gathered_two, row_hits(gathered_two.shape[0], all_leaving), moved)

    groups = key_cache.shape[2] // HEAD_DIM
    chunks = next(n for n in (CHUNKS, 1) if groups % n == 0)
    (sums_one,), last_sent = project_sums(lined_one, w_qkv, 1)
    sums_two, _ = project_sums(line_up(gathered_two), w_qkv, chunks, last_sent)
    attended_one, new_one = attend(sums_one, turn_tables(own_lengths), (), key_cache, value_cache, own_lengths, 0, 1)
    tables_two = turn_tables(own_lengths + 1)
    attended_two = [
        attend(part, tables_two, (new_one,), key_cache, value_cache, own_lengths, c, chunks)[0]
        for c, part in enumerate(sums_two)
    ]

    leaving, _, came_from = own_slots(mig_rows, dest)
    leave_hits = row_hits(row_count, leaving)
    sent = jnp.concatenate([pick_rows(leave_hits.T, part) for part in attended_two], axis=1)
    returned = pick_rows(partner_hits(came_from), all_replicas(sent))
    if not pairwise():
        table = replace_rows(jnp.concatenate(attended_two, axis=1), leave_hits, returned)
        return (mix_rows(attended_one, w_out), mix_rows(table, w_out))
    out_one = mix_lined([by_side(spread_rows(attended_one), row_count)], w_out)
    slots, width = returned.shape[0], attended_two[0].shape[1]
    held, bit = returned, lax.axis_size("gx") // 2
    while bit > 1:
        held = jnp.concatenate([held, swap(held, "gx", bit)], axis=0)
        bit //= 2
    extra = jnp.concatenate([held[:, c * width : (c + 1) * width] for c in range(chunks)], axis=0)
    lined = [spread_rows(part) for part in attended_two[:-1]]
    last, extra = spread_rows(attended_two[-1], extra)
    lined = [by_side(part, row_count) for part in lined + [last]]
    extra = extra.reshape(2, chunks, held.shape[0], width)
    fixed = [by_side(extra[:, c].reshape(-1, width), slots) for c in range(chunks)]
    half_slots, half_rows = all_leaving.shape[0] // 2, lined[0].shape[0] // 2
    lined_slots = jnp.where(
        lax.axis_index("gy") == 0,
        jnp.concatenate([all_leaving[half_slots:] - half_rows, all_leaving[:half_slots] + half_rows]),
        all_leaving,
    )
    hits = row_hits(2 * half_rows, lined_slots)
    lined = [lax.optimization_barrier(replace_rows(part, hits, rows)) for part, rows in zip(lined, fixed)]
    return (out_one, mix_lined(lined, w_out))


def solution(mesh):
    placed = (
        P(("rep", "gy"), "gx"),
        P(("rep", "gy"), "gx"),
        P("gx", "gy"),
        P("gy", "gx"),
        P(("rep", "gx"), None, "gy"),
        P(("rep", "gx"), None, "gy"),
        P(None, "gx"),
        P(None, "gx", None),
        P(None, "gx", None),
    )
    return jax.shard_map(
        steps,
        mesh=mesh,
        in_specs=placed,
        out_specs=(P(("rep", "gy"), "gx"), P(("rep", "gy"), "gx")),
        check_vma=False,
    )
```

time: 193 us -> 165 us (0.85)
  waiting for transfers between devices: 72.4 us -> 94.1 us
  other arithmetic: 27.1 us -> 7.18 us
  matrix products: 39.8 us -> 20 us
  between operations: 19 us -> 1.27 us
  Pallas kernels: 0 us -> 9.43 us
  local copies, waits for them, and re-layouts: 10.4 us -> 8.05 us
    dot_general x8 -> x14, matrix products: 39.8 us -> 20 us  [the longest x3 11.7 us: project_sums(): parts.append(jnp.dot(lined, weights, preferred_element_type=jnp.float32))]
    ppermute x12 -> x20, waiting for transfers between devices: 72.4 us -> 92 us  [swap(): return lax.ppermute(value, axis, [(i, i ^ bit) for i in range(count)])]
    pallas_call x0 -> x3, Pallas kernels: none -> 9.43 us  [attend(): pl.pallas_call(attend_block, grid_spec=pltpu.PrefetchScalarGridSpec(num_s...]
    eq x5 -> x1, other arithmetic: 4.88 us -> 0.01 us  [table_of_all(): jnp.arange(count, dtype=jnp.int32) == lax.axis_index('gx')]
    ppermute x12 -> x20, starting transfers between devices: 18.5 us -> 21.9 us  [swap(): return lax.ppermute(value, axis, [(i, i ^ bit) for i in range(count)])]
    select_n x9 -> x4, other arithmetic: 3.57 us -> 0.23 us  [the longest x2 0.08 us: gather_rows(): jnp.where(first, hidden, peer)]
    unnamed x40 -> x20, local copies, waits for them, and re-layouts: 2.1 us -> 4.85 us
    reduce_sum x5 -> x1, other arithmetic: 3.31 us -> 0.82 us  [own_slots(): came_from = jnp.sum(jnp.where(dest == replica, ids, 0), axis=0).reshape(-1)]
  transfers between devices with their start and end apart: 18 -> 26, of which waited for: 9 -> 14; matrix products, arithmetic and copies ran while one was open for 31% -> 15% of each run, Pallas kernels for 0% -> 0%
where the time goes in v2:
time: 165 us
  waiting for transfers between devices  94.1 us (57%)
  starting transfers between devices  25.1 us (15%)
  matrix products  20 us (12%)
  Pallas kernels  9.43 us (6%)
  local copies, waits for them, and re-layouts  8.05 us (5%)
  other arithmetic  7.18 us (4%)
    ppermute x20, waiting for transfers between devices, swap(): return lax.ppermute(value, axis, [(i, i ^ bit) for i in range(count)])  92 us
    ppermute x20, starting transfers between devices, swap(): return lax.ppermute(value, axis, [(i, i ^ bit) for i in range(count)])  21.9 us
    dot_general x3, matrix products, project_sums(): parts.append(jnp.dot(lined, weights, preferred_element_type=jnp.float32))  11.7 us
    pallas_call x3, Pallas kernels, attend(): pl.pallas_call(attend_block, grid_spec=pltpu.PrefetchScalarGridSpec(num_s...  9.43 us
    dot_general x3, matrix products, mix_lined(): piece = jnp.dot(part, weights, preferred_element_type=jnp.float32)  5.04 us
    unnamed x20, local copies, waits for them, and re-layouts  4.85 us
  transfers between devices with their start and end apart: 26, of which 14 were waited for; matrix products, arithmetic and copies ran while one was open for 15% of the time, Pallas kernels for 0%

profile of v2, /device:TPU:0, one launch (start us, length us, event | category | flops | bytes accessed | tf_op | source)
XLA Modules:
  0.0 165.1 jit_solution(3138082161818116675)
XLA Ops:
  0.6 3.0 %collective-permute-start = (bf16[64,2048]{1,0:T(8,128)(2,1)}, bf16[64,2048]{1,0:T(8,128)(2,1)S(1)}, u32[]{:S(2)}, u32[]{:S(2)}) collective-permute-start(bf16[64,2048]{1,0:T(8,128)(2,1)} %param.9), channel_id=1, source_target_pairs={{0,1},{1,0},{2,3},{3,2},{4,5},{5,4},{6,7},{7,6},{8,9},{9,8},{10,11... | collective-permute-start | bytes 786440 | tf_op jit(solution)/shard_map/ppermute | solution.py:25
  3.7 0.7 pad_add_fusion
  4.5 2.0 %collective-permute-start.6 = (s32[2,4,4,2,2]{1,3,2,4,0:T(2,128)S(1)}, s32[2,4,4,2,2]{1,3,2,4,0:T(2,128)S(1)}, u32[]{:S(2)}, u32[]{:S(2)}) collective-permute-start(s32[2,4,4,2,2]{1,3,2,4,0:T(2,128)S(1)} %broadcast_select_fusion.6), channel_id=1, source_target_pairs={{0,2},{2,0},{4,6},{6,4},{1,3},{3,1},{5,7},{7,5},{8,10},{10,8},{12,... | collective-permute-start | bytes 1544 | tf_op jit(solution)/shard_map/ppermute | solution.py:25
  6.6 0.8 fusion.80
  7.4 0.7 add_convert_fusion
  9.1 0.9 fusion.81
  10.1 2.6 %collective-permute-start.7 = (s32[2,4,4,2,2]{1,3,2,4,0:T(2,128)S(1)}, s32[2,4,4,2,2]{1,3,2,4,0:T(2,128)S(1)}, u32[]{:S(2)}, u32[]{:S(2)}) collective-permute-start(s32[2,4,4,2,2]{1,3,2,4,0:T(2,128)S(1)} %fusion.99), channel_id=1, source_target_pairs={{0,4},{2,6},{4,0},{6,2},{1,5},{3,7},{5,1},{7,3},{8,12},{10,14},{12... | collective-permute-start | bytes 1544 | tf_op jit(solution)/shard_map/ppermute | solution.py:25
  12.7 2.0 %collective-permute-done.7 = s32[2,4,4,2,2]{1,3,2,4,0:T(2,128)S(1)} collective-permute-done((s32[2,4,4,2,2]{1,3,2,4,0:T(2,128)S(1)}, s32[2,4,4,2,2]{1,3,2,4,0:T(2,128)S(1)}, u32[]{:S(2)}, u32[]{:S(2)}) %collective-permute-start.7) | collective-permute-done | bytes 544 | tf_op jit(solution)/shard_map/ppermute | solution.py:25
  15.2 1.2 convolution_convert_fusion.5
  16.3 1.6 collective-permute-start.9
  19.4 1.1 collective-permute-done.9
  20.5 0.8 collective-permute-done.8
  21.5 1.5 collective-permute-start.11
  23.0 1.0 broadcast_select_fusion.2
  24.4 8.7 %fusion.100 = f32[128,5120]{1,0:T(8,128)S(1)} fusion(bf16[2048,5120]{1,0:T(8,128)(2,1)} %param.11, bf16[32,2048]{1,0:T(8,128)(2,1)S(1)} %get-tuple-element.49, bf16[32,2048]{1,0:T(8,128)(2,1)S(1)} %get-tuple-element.48, bf16[32,2048]{1,0:T(8,128)(2,1)S(1)} %get-tuple-element.47, bf16[32,2048]{1,0:T(8,128)(2,1)S(1)} %get-tuple-element.46), kind=kOutput, calls=%fused_computation.217 | convolution fusion | flops 2686451712 | bytes 24117248 | tf_op jit(solution)/shard_map/dot_general | solution.py:67
  33.2 0.4 fusion.11
  33.7 3.7 %copy-done.2 = bf16[2048,5120]{1,0:T(8,128)(2,1)S(1)} copy-done((bf16[2048,5120]{1,0:T(8,128)(2,1)S(1)}, bf16[2048,5120]{1,0:T(8,128)(2,1)}, u32[]{:S(2)}) %copy-start.2) | copy-done | bytes 20971544
  37.4 1.5 fusion
  38.9 1.5 fusion.2
  40.6 0.5 collective-permute-start.1
  41.1 1.7 %collective-permute-start.15 = (f16[64,2560]{1,0:T(8,128)(2,1)S(1)}, f16[64,2560]{1,0:T(8,128)(2,1)S(1)}, u32[]{:S(2)}, u32[]{:S(2)}) collective-permute-start(f16[64,2560]{1,0:T(8,128)(2,1)S(1)} %fusion.22), channel_id=1, source_target_pairs={{0,2},{2,0},{4,6},{6,4},{1,3},{3,1},{5,7},{7,5},{8,10},{10,8},{12,... | collective-permute-start | bytes 983048 | tf_op jit(solution)/shard_map/ppermute | solution.py:25
  42.9 0.5 collective-permute-start.13
  43.3 18.4 %collective-permute-done.1 = f16[64,5120]{1,0:T(8,128)(2,1)S(1)} collective-permute-done((f16[64,5120]{1,0:T(8,128)(2,1)S(1)}, f16[64,5120]{1,0:T(8,128)(2,1)S(1)}, u32[]{:S(2)}, u32[]{:S(2)}) %collective-permute-start.1) | collective-permute-done | bytes 655392 | tf_op jit(solution)/shard_map/ppermute | solution.py:25
  62.0 0.4 collective-permute-start.2
  62.4 11.6 %collective-permute-done.15 = f16[64,2560]{1,0:T(8,128)(2,1)S(1)} collective-permute-done((f16[64,2560]{1,0:T(8,128)(2,1)S(1)}, f16[64,2560]{1,0:T(8,128)(2,1)S(1)}, u32[]{:S(2)}, u32[]{:S(2)}) %collective-permute-start.15) | collective-permute-done | bytes 327712 | tf_op jit(solution)/shard_map/ppermute | solution.py:25
  74.3 4.5 %collective-permute-done.13 = f16[64,2560]{1,0:T(8,128)(2,1)S(1)} collective-permute-done((f16[64,2560]{1,0:T(8,128)(2,1)S(1)}, f16[64,2560]{1,0:T(8,128)(2,1)S(1)}, u32[]{:S(2)}, u32[]{:S(2)}) %collective-permute-start.13) | collective-permute-done | bytes 327712 | tf_op jit(solution)/shard_map/ppermute | solution.py:25
  79.0 10.4 %collective-permute-done.16 = f16[32,2560]{1,0:T(8,128)(2,1)S(1)} collective-permute-done((f16[32,2560]{1,0:T(8,128)(2,1)S(1)}, f16[32,2560]{1,0:T(8,128)(2,1)S(1)}, u32[]{:S(2)}, u32[]{:S(2)}) %collective-permute-start.16) | collective-permute-done | bytes 163872 | tf_op jit(solution)/shard_map/ppermute | solution.py:25
  89.5 1.8 %collective-permute-done.14 = f16[32,2560]{1,0:T(8,128)(2,1)S(1)} collective-permute-done((f16[32,2560]{1,0:T(8,128)(2,1)S(1)}, f16[32,2560]{1,0:T(8,128)(2,1)S(1)}, u32[]{:S(2)}, u32[]{:S(2)}) %collective-permute-start.14) | collective-permute-done | bytes 163872 | tf_op jit(solution)/shard_map/ppermute | solution.py:25
  91.5 3.7 %shard_map.104 = (bf16[32,4096]{1,0:T(8,128)(2,1)S(1)}, f32[32,1024]{1,0:T(8,128)S(1)}) custom-call(s32[32]{0:T(128)S(1)} %get-tuple-element.27.lengths, f32[32,5120]{1,0:T(8,128)S(1)} %slice_add_fusion.3.sums, f32[32,128]{1,0:T(8,128)S(1)} %get-tuple-element.79.cosine, f32[32,128]{1,0:T(8,128)S(1)} %get-tuple-element.80.sine, ...), custom_call_target="tpu_custom_call" | custom-call | flops 536870912 | bytes 8388608 | tf_op jit(solution)/shard_map/pallas_call | solution.py:180
  95.2 2.9 %shard_map.106 = (bf16[32,2048]{1,0:T(8,128)(2,1)S(1)}, f32[32,512]{1,0:T(8,128)}) custom-call(s32[32]{0:T(128)S(1)} %get-tuple-element.27.lengths, f32[32,2560]{1,0:T(8,128)S(1)} %slice_add_fusion.6.sums, f32[32,128]{1,0:T(8,128)S(1)} %get-tuple-element.81.cosine, f32[32,128]{1,0:T(8,128)S(1)} %get-tuple-element.82.sine, ...), custom_call_target="tpu_custom_call" | custom-call | flops 134217728 | bytes 4194304 | tf_op jit(solution)/shard_map/pallas_call | solution.py:180
  98.1 2.9 %shard_map.105 = (bf16[32,2048]{1,0:T(8,128)(2,1)S(1)}, f32[32,512]{1,0:T(8,128)}) custom-call(s32[32]{0:T(128)S(1)} %get-tuple-element.27.lengths, f32[32,2560]{1,0:T(8,128)S(1)} %slice_add_fusion.7.sums, f32[32,128]{1,0:T(8,128)S(1)} %get-tuple-element.81.cosine, f32[32,128]{1,0:T(8,128)S(1)} %get-tuple-element.82.sine, ...), custom_call_target="tpu_custom_call" | custom-call | flops 134217728 | bytes 4194304 | tf_op jit(solution)/shard_map/pallas_call | solution.py:180
  101.4 1.2 collective-permute-start.18
  102.9 2.9 %collective-permute-start.21 = (bf16[32,2048]{1,0:T(8,128)(2,1)S(1)}, bf16[32,2048]{1,0:T(8,128)(2,1)S(1)}, u32[]{:S(2)}, u32[]{:S(2)}) collective-permute-start(bf16[32,2048]{1,0:T(8,128)(2,1)S(1)} %get-tuple-element.21), channel_id=1, source_target_pairs={{0,4},{2,6},{4,0},{6,2},{1,5},{3,7},{5,1},{7,3},{8,12},{10,14},{12... | collective-permute-start | bytes 393224 | tf_op jit(solution)/shard_map/ppermute | solution.py:25
  106.2 3.0 %collective-permute-start.23 = (bf16[32,2048]{1,0:T(8,128)(2,1)S(1)}, bf16[32,2048]{1,0:T(8,128)(2,1)S(1)}, u32[]{:S(2)}, u32[]{:S(2)}) collective-permute-start(bf16[32,2048]{1,0:T(8,128)(2,1)S(1)} %get-tuple-element.18), channel_id=1, source_target_pairs={{0,4},{2,6},{4,0},{6,2},{1,5},{3,7},{5,1},{7,3},{8,12},{10,14},{12... | collective-permute-start | bytes 393224 | tf_op jit(solution)/shard_map/ppermute | solution.py:25
  109.2 18.2 %collective-permute-done.20 = bf16[4,4096]{1,0:T(4,128)(2,1)S(1)} collective-permute-done((bf16[4,4096]{1,0:T(4,128)(2,1)S(1)}, bf16[4,4096]{1,0:T(4,128)(2,1)S(1)}, u32[]{:S(2)}, u32[]{:S(2)}) %collective-permute-start.20) | collective-permute-done | bytes 32800 | tf_op jit(solution)/shard_map/ppermute | solution.py:25
  127.6 2.6 %collective-permute-done.23 = bf16[32,2048]{1,0:T(8,128)(2,1)S(1)} collective-permute-done((bf16[32,2048]{1,0:T(8,128)(2,1)S(1)}, bf16[32,2048]{1,0:T(8,128)(2,1)S(1)}, u32[]{:S(2)}, u32[]{:S(2)}) %collective-permute-start.23) | collective-permute-done | bytes 131104 | tf_op jit(solution)/shard_map/ppermute | solution.py:25
  130.4 2.1 %collective-permute-start.4 = (bf16[64,4096]{1,0:T(8,128)(2,1)S(1)}, bf16[64,4096]{1,0:T(8,128)(2,1)S(1)}, u32[]{:S(2)}, u32[]{:S(2)}) collective-permute-start(bf16[64,4096]{1,0:T(8,128)(2,1)S(1)} %pad_maximum_fusion.1), channel_id=1, source_target_pairs={{0,2},{2,0},{4,6},{6,4},{1,3},{3,1},{5,7},{7,5},{8,10},{10,8},{12,... | collective-permute-start | bytes 1572872 | tf_op jit(solution)/shard_map/ppermute | solution.py:25
  132.5 11.3 %collective-permute-done.24 = bf16[64,2048]{1,0:T(8,128)(2,1)S(1)} collective-permute-done((bf16[64,2048]{1,0:T(8,128)(2,1)S(1)}, bf16[64,2048]{1,0:T(8,128)(2,1)S(1)}, u32[]{:S(2)}, u32[]{:S(2)}) %collective-permute-start.24) | collective-permute-done | bytes 262176 | tf_op jit(solution)/shard_map/ppermute | solution.py:25
  145.1 1.0 slice-done.3
  146.1 1.3 fusion.4
  147.4 1.3 fusion.8
  148.8 0.6 collective-permute-start.25
  149.4 4.8 %collective-permute-done.4 = bf16[64,4096]{1,0:T(8,128)(2,1)S(1)} collective-permute-done((bf16[64,4096]{1,0:T(8,128)(2,1)S(1)}, bf16[64,4096]{1,0:T(8,128)(2,1)S(1)}, u32[]{:S(2)}, u32[]{:S(2)}) %collective-permute-start.4) | collective-permute-done | bytes 524320 | tf_op jit(solution)/shard_map/ppermute | solution.py:25
  154.3 2.4 %fusion.14 = f32[128,2048]{1,0:T(8,128)S(1)} fusion(bf16[4096,2048]{1,0:T(8,128)(2,1)S(1)} %bitcast.25, bf16[32,4096]{1,0:T(8,128)(2,1)S(1)} %get-tuple-element.29, bf16[32,4096]{1,0:T(8,128)(2,1)S(1)} %get-tuple-element.30, bf16[32,4096]{1,0:T(8,128)(2,1)S(1)} %get-tuple-element.31, bf16[32,4096]{1,0:T(8,128)(2,1)S(1)} %get-tuple-element.28), kind=kOutput, calls=%fused_computation.22 | convolution fusion | flops 2151677952 | bytes 18874368 | tf_op jit(solution)/shard_map/dot_general | solution.py:254
  156.8 0.6 collective-permute-start.5
  157.4 0.8 fusion.25
  158.1 6.2 %collective-permute-done.5 = bf16[64,2048]{1,0:T(8,128)(2,1)S(1)} collective-permute-done((bf16[64,2048]{1,0:T(8,128)(2,1)S(1)}, bf16[64,2048]{1,0:T(8,128)(2,1)S(1)}, u32[]{:S(2)}, u32[]{:S(2)}) %collective-permute-start.5) | collective-permute-done | bytes 262176 | tf_op jit(solution)/shard_map/ppermute | solution.py:25
  164.3 0.8 fusion.26
  (127 shorter events, 7.6 us)
Async XLA Ops:
  0.6 22.4 %collective-permute-start = (bf16[64,2048]{1,0:T(8,128)(2,1)}, bf16[64,2048]{1,0:T(8,128)(2,1)S(1)}, u32[]{:S(2)}, u32[]{:S(2)}) collective-permute-start(bf16[64,2048]{1,0:T(8,128)(2,1)} %param.9), channel_id=1, source_target_pairs={{0,1},{1,0},{2,3},{3,2},{4,5},{5,4},{6,7},{7,6},{8,9},{9,8},{10,11... | collective-permute-start | bytes 786440 | tf_op jit(solution)/shard_map/ppermute | solution.py:25
  3.7 29.4 %collective-permute-start.12 = (bf16[64,2048]{1,0:T(8,128)(2,1)}, bf16[64,2048]{1,0:T(8,128)(2,1)S(1)}, u32[]{:S(2)}, u32[]{:S(2)}) collective-permute-start(bf16[64,2048]{1,0:T(8,128)(2,1)} %param.10), channel_id=1, source_target_pairs={{0,1},{1,0},{2,3},{3,2},{4,5},{5,4},{6,7},{7,6},{8,9},{9,8},{10,11... | collective-permute-start | bytes 786440 | tf_op jit(solution)/shard_map/ppermute | solution.py:25
  4.5 5.5 %collective-permute-start.6 = (s32[2,4,4,2,2]{1,3,2,4,0:T(2,128)S(1)}, s32[2,4,4,2,2]{1,3,2,4,0:T(2,128)S(1)}, u32[]{:S(2)}, u32[]{:S(2)}) collective-permute-start(s32[2,4,4,2,2]{1,3,2,4,0:T(2,128)S(1)} %broadcast_select_fusion.6), channel_id=1, source_target_pairs={{0,2},{2,0},{4,6},{6,4},{1,3},{3,1},{5,7},{7,5},{8,10},{10,8},{12,... | collective-permute-start | bytes 1544 | tf_op jit(solution)/shard_map/ppermute | solution.py:25
  10.1 4.7 %collective-permute-start.7 = (s32[2,4,4,2,2]{1,3,2,4,0:T(2,128)S(1)}, s32[2,4,4,2,2]{1,3,2,4,0:T(2,128)S(1)}, u32[]{:S(2)}, u32[]{:S(2)}) collective-permute-start(s32[2,4,4,2,2]{1,3,2,4,0:T(2,128)S(1)} %fusion.99), channel_id=1, source_target_pairs={{0,4},{2,6},{4,0},{6,2},{1,5},{3,7},{5,1},{7,3},{8,12},{10,14},{12... | collective-permute-start | bytes 1544 | tf_op jit(solution)/shard_map/ppermute | solution.py:25
  16.3 3.1 %collective-permute-start.10 = (bf16[8,2048]{1,0:T(8,128)(2,1)S(1)}, bf16[8,2048]{1,0:T(8,128)(2,1)S(1)}, u32[]{:S(2)}, u32[]{:S(2)}) collective-permute-start(bf16[8,2048]{1,0:T(8,128)(2,1)S(1)} %convolution_convert_fusion.5), channel_id=1, source_target_pairs={{0,24},{8,0},{16,8},{24,16},{1,25},{9,1},{17,9},{25,17},{2,26},{10... | collective-permute-start | bytes 98312 | tf_op jit(solution)/shard_map/ppermute | solution.py:270
  16.3 4.1 %collective-permute-start.9 = (bf16[8,2048]{1,0:T(8,128)(2,1)S(1)}, bf16[8,2048]{1,0:T(8,128)(2,1)S(1)}, u32[]{:S(2)}, u32[]{:S(2)}) collective-permute-start(bf16[8,2048]{1,0:T(8,128)(2,1)S(1)} %convolution_convert_fusion.5), channel_id=1, source_target_pairs={{0,16},{8,24},{16,0},{24,8},{1,17},{9,25},{17,1},{25,9},{2,18},{10... | collective-permute-start | bytes 98312 | tf_op jit(solution)/shard_map/ppermute | solution.py:270
  18.0 3.3 %collective-permute-start.8 = (bf16[8,2048]{1,0:T(8,128)(2,1)S(1)}, bf16[8,2048]{1,0:T(8,128)(2,1)S(1)}, u32[]{:S(2)}, u32[]{:S(2)}) collective-permute-start(bf16[8,2048]{1,0:T(8,128)(2,1)S(1)} %convolution_convert_fusion.5), channel_id=1, source_target_pairs={{0,8},{8,16},{16,24},{24,0},{1,9},{9,17},{17,25},{25,1},{2,10},{10... | collective-permute-start | bytes 98312 | tf_op jit(solution)/shard_map/ppermute | solution.py:270
  21.5 11.7 %collective-permute-start.11 = (bf16[8,2048]{1,0:T(8,128)(2,1)S(1)}, bf16[8,2048]{1,0:T(8,128)(2,1)S(1)}, u32[]{:S(2)}, u32[]{:S(2)}) collective-permute-start(bf16[8,2048]{1,0:T(8,128)(2,1)S(1)} %convolution_convert_fusion.4), channel_id=1, source_target_pairs={{0,1},{1,0},{2,3},{3,2},{4,5},{5,4},{6,7},{7,6},{8,9},{9,8},{10,11... | collective-permute-start | bytes 98312 | tf_op jit(solution)/shard_map/ppermute | solution.py:25
  24.4 8.7 %copy-start.3 = (bf16[64,2048]{1,0:T(8,128)(2,1)S(1)}, bf16[64,2048]{1,0:T(8,128)(2,1)}, u32[]{:S(2)}) copy-start(bf16[64,2048]{1,0:T(8,128)(2,1)} %param.10) | copy-start | bytes 786436
  24.4 13.0 %copy-start.2 = (bf16[2048,5120]{1,0:T(8,128)(2,1)S(1)}, bf16[2048,5120]{1,0:T(8,128)(2,1)}, u32[]{:S(2)}) copy-start(bf16[2048,5120]{1,0:T(8,128)(2,1)} %param.11) | copy-start | bytes 62914564
  40.6 21.2 %collective-permute-start.1 = (f16[64,5120]{1,0:T(8,128)(2,1)S(1)}, f16[64,5120]{1,0:T(8,128)(2,1)S(1)}, u32[]{:S(2)}, u32[]{:S(2)}) collective-permute-start(f16[64,5120]{1,0:T(8,128)(2,1)S(1)} %fusion.13), channel_id=1, source_target_pairs={{0,2},{2,0},{4,6},{6,4},{1,3},{3,1},{5,7},{7,5},{8,10},{10,8},{12,... | collective-permute-start | bytes 1966088 | tf_op jit(solution)/shard_map/ppermute | solution.py:25
  41.1 33.0 %collective-permute-start.15 = (f16[64,2560]{1,0:T(8,128)(2,1)S(1)}, f16[64,2560]{1,0:T(8,128)(2,1)S(1)}, u32[]{:S(2)}, u32[]{:S(2)}) collective-permute-start(f16[64,2560]{1,0:T(8,128)(2,1)S(1)} %fusion.22), channel_id=1, source_target_pairs={{0,2},{2,0},{4,6},{6,4},{1,3},{3,1},{5,7},{7,5},{8,10},{10,8},{12,... | collective-permute-start | bytes 983048 | tf_op jit(solution)/shard_map/ppermute | solution.py:25
  42.9 36.0 %collective-permute-start.13 = (f16[64,2560]{1,0:T(8,128)(2,1)S(1)}, f16[64,2560]{1,0:T(8,128)(2,1)S(1)}, u32[]{:S(2)}, u32[]{:S(2)}) collective-permute-start(f16[64,2560]{1,0:T(8,128)(2,1)S(1)} %fusion.23), channel_id=1, source_target_pairs={{0,2},{2,0},{4,6},{6,4},{1,3},{3,1},{5,7},{7,5},{8,10},{10,8},{12,... | collective-permute-start | bytes 983048 | tf_op jit(solution)/shard_map/ppermute | solution.py:25
  61.9 29.5 %copy-start.1 = (bf16[32,128,512]{2,1,0:T(8,128)(2,1)S(1)}, bf16[32,128,512]{2,1,0:T(8,128)(2,1)}, u32[]{:S(2)}) copy-start(bf16[32,128,512]{2,1,0:T(8,128)(2,1)} %rest_2_.3) | copy-start | bytes 12582916
  62.0 29.4 %collective-permute-start.2 = (f16[32,5120]{1,0:T(8,128)(2,1)S(1)}, f16[32,5120]{1,0:T(8,128)(2,1)S(1)}, u32[]{:S(2)}, u32[]{:S(2)}) collective-permute-start(f16[32,5120]{1,0:T(8,128)(2,1)S(1)} %fusion.24), channel_id=1, source_target_pairs={{0,4},{2,6},{4,0},{6,2},{1,5},{3,7},{5,1},{7,3},{8,12},{10,14},{12... | collective-permute-start | bytes 983048 | tf_op jit(solution)/shard_map/ppermute | solution.py:25
  74.2 17.3 %copy-start = (bf16[32,128,512]{2,1,0:T(8,128)(2,1)S(1)}, bf16[32,128,512]{2,1,0:T(8,128)(2,1)}, u32[]{:S(2)}) copy-start(bf16[32,128,512]{2,1,0:T(8,128)(2,1)} %rest_1_.5) | copy-start | bytes 12582916
  74.2 15.3 %collective-permute-start.16 = (f16[32,2560]{1,0:T(8,128)(2,1)S(1)}, f16[32,2560]{1,0:T(8,128)(2,1)S(1)}, u32[]{:S(2)}, u32[]{:S(2)}) collective-permute-start(f16[32,2560]{1,0:T(8,128)(2,1)S(1)} %fusion.27), channel_id=1, source_target_pairs={{0,4},{2,6},{4,0},{6,2},{1,5},{3,7},{5,1},{7,3},{8,12},{10,14},{12... | collective-permute-start | bytes 491528 | tf_op jit(solution)/shard_map/ppermute | solution.py:25
  79.0 12.3 %collective-permute-start.14 = (f16[32,2560]{1,0:T(8,128)(2,1)S(1)}, f16[32,2560]{1,0:T(8,128)(2,1)S(1)}, u32[]{:S(2)}, u32[]{:S(2)}) collective-permute-start(f16[32,2560]{1,0:T(8,128)(2,1)S(1)} %fusion.28), channel_id=1, source_target_pairs={{0,4},{2,6},{4,0},{6,2},{1,5},{3,7},{5,1},{7,3},{8,12},{10,14},{12... | collective-permute-start | bytes 491528 | tf_op jit(solution)/shard_map/ppermute | solution.py:25
  95.1 49.9 %slice-start = ((s8[16777216]{0:T(1024)(128)(4,1)}), s8[4194304]{0:T(1024)(128)(4,1)S(1)}, s32[]{:S(2)}) async-start(s8[16777216]{0:T(1024)(128)(4,1)} %bitcast.24), calls=%async_computation | async-start | bytes 8388608
  95.2 49.9 %slice-start.1 = ((s8[16777216]{0:T(1024)(128)(4,1)}), s8[4194304]{0:T(1024)(128)(4,1)S(1)}, s32[]{:S(2)}) async-start(s8[16777216]{0:T(1024)(128)(4,1)} %bitcast.24), calls=%async_computation.1 | async-start | bytes 8388608
  98.1 47.0 %slice-start.2 = ((s8[16777216]{0:T(1024)(128)(4,1)}), s8[4194304]{0:T(1024)(128)(4,1)S(1)}, s32[]{:S(2)}) async-start(s8[16777216]{0:T(1024)(128)(4,1)} %bitcast.24), calls=%async_computation.2 | async-start | bytes 8388608
  101.4 4.4 %collective-permute-start.19 = (bf16[4,4096]{1,0:T(4,128)(2,1)S(1)}, bf16[4,4096]{1,0:T(4,128)(2,1)S(1)}, u32[]{:S(2)}, u32[]{:S(2)}) collective-permute-start(bf16[4,4096]{1,0:T(4,128)(2,1)S(1)} %pad_maximum_fusion.10), channel_id=1, source_target_pairs={{0,24},{8,0},{16,8},{24,16},{1,25},{9,1},{17,9},{25,17},{2,26},{10... | collective-permute-start | bytes 98312 | tf_op jit(solution)/shard_map/ppermute | solution.py:270
  101.4 4.3 %collective-permute-start.18 = (bf16[4,4096]{1,0:T(4,128)(2,1)S(1)}, bf16[4,4096]{1,0:T(4,128)(2,1)S(1)}, u32[]{:S(2)}, u32[]{:S(2)}) collective-permute-start(bf16[4,4096]{1,0:T(4,128)(2,1)S(1)} %pad_maximum_fusion.10), channel_id=1, source_target_pairs={{0,16},{8,24},{16,0},{24,8},{1,17},{9,25},{17,1},{25,9},{2,18},{10... | collective-permute-start | bytes 98312 | tf_op jit(solution)/shard_map/ppermute | solution.py:270
  102.6 3.3 %collective-permute-start.17 = (bf16[4,4096]{1,0:T(4,128)(2,1)S(1)}, bf16[4,4096]{1,0:T(4,128)(2,1)S(1)}, u32[]{:S(2)}, u32[]{:S(2)}) collective-permute-start(bf16[4,4096]{1,0:T(4,128)(2,1)S(1)} %pad_maximum_fusion.10), channel_id=1, source_target_pairs={{0,8},{8,16},{16,24},{24,0},{1,9},{9,17},{17,25},{25,1},{2,10},{10... | collective-permute-start | bytes 98312 | tf_op jit(solution)/shard_map/ppermute | solution.py:270
  102.8 27.6 %collective-permute-start.3 = (bf16[32,4096]{1,0:T(8,128)(2,1)S(1)}, bf16[32,4096]{1,0:T(8,128)(2,1)S(1)}, u32[]{:S(2)}, u32[]{:S(2)}) collective-permute-start(bf16[32,4096]{1,0:T(8,128)(2,1)S(1)} %get-tuple-element.12), channel_id=1, source_target_pairs={{0,4},{2,6},{4,0},{6,2},{1,5},{3,7},{5,1},{7,3},{8,12},{10,14},{12... | collective-permute-start | bytes 786440 | tf_op jit(solution)/shard_map/ppermute | solution.py:25
  102.9 24.6 %collective-permute-start.21 = (bf16[32,2048]{1,0:T(8,128)(2,1)S(1)}, bf16[32,2048]{1,0:T(8,128)(2,1)S(1)}, u32[]{:S(2)}, u32[]{:S(2)}) collective-permute-start(bf16[32,2048]{1,0:T(8,128)(2,1)S(1)} %get-tuple-element.21), channel_id=1, source_target_pairs={{0,4},{2,6},{4,0},{6,2},{1,5},{3,7},{5,1},{7,3},{8,12},{10,14},{12... | collective-permute-start | bytes 393224 | tf_op jit(solution)/shard_map/ppermute | solution.py:25
  106.2 21.3 %collective-permute-start.20 = (bf16[4,4096]{1,0:T(4,128)(2,1)S(1)}, bf16[4,4096]{1,0:T(4,128)(2,1)S(1)}, u32[]{:S(2)}, u32[]{:S(2)}) collective-permute-start(bf16[4,4096]{1,0:T(4,128)(2,1)S(1)} %convolution_convert_fusion), channel_id=1, source_target_pairs={{0,4},{2,6},{4,0},{6,2},{1,5},{3,7},{5,1},{7,3},{8,12},{10,14},{12... | collective-permute-start | bytes 98312 | tf_op jit(solution)/shard_map/ppermute | solution.py:25
  106.2 24.0 %collective-permute-start.23 = (bf16[32,2048]{1,0:T(8,128)(2,1)S(1)}, bf16[32,2048]{1,0:T(8,128)(2,1)S(1)}, u32[]{:S(2)}, u32[]{:S(2)}) collective-permute-start(bf16[32,2048]{1,0:T(8,128)(2,1)S(1)} %get-tuple-element.18), channel_id=1, source_target_pairs={{0,4},{2,6},{4,0},{6,2},{1,5},{3,7},{5,1},{7,3},{8,12},{10,14},{12... | collective-permute-start | bytes 393224 | tf_op jit(solution)/shard_map/ppermute | solution.py:25
  127.5 16.3 %collective-permute-start.22 = (bf16[80,2048]{1,0:T(8,128)(2,1)S(1)}, bf16[80,2048]{1,0:T(8,128)(2,1)S(1)}, u32[]{:S(2)}, u32[]{:S(2)}) collective-permute-start(bf16[80,2048]{1,0:T(8,128)(2,1)S(1)} %pad_maximum_fusion.4), channel_id=1, source_target_pairs={{0,2},{2,0},{4,6},{6,4},{1,3},{3,1},{5,7},{7,5},{8,10},{10,8},{12,... | collective-permute-start | bytes 983048 | tf_op jit(solution)/shard_map/ppermute | solution.py:25
  130.3 13.5 %collective-permute-start.24 = (bf16[64,2048]{1,0:T(8,128)(2,1)S(1)}, bf16[64,2048]{1,0:T(8,128)(2,1)S(1)}, u32[]{:S(2)}, u32[]{:S(2)}) collective-permute-start(bf16[64,2048]{1,0:T(8,128)(2,1)S(1)} %pad_maximum_fusion.5), channel_id=1, source_target_pairs={{0,2},{2,0},{4,6},{6,4},{1,3},{3,1},{5,7},{7,5},{8,10},{10,8},{12,... | collective-permute-start | bytes 786440 | tf_op jit(solution)/shard_map/ppermute | solution.py:25
  130.4 23.7 %collective-permute-start.4 = (bf16[64,4096]{1,0:T(8,128)(2,1)S(1)}, bf16[64,4096]{1,0:T(8,128)(2,1)S(1)}, u32[]{:S(2)}, u32[]{:S(2)}) collective-permute-start(bf16[64,4096]{1,0:T(8,128)(2,1)S(1)} %pad_maximum_fusion.1), channel_id=1, source_target_pairs={{0,2},{2,0},{4,6},{6,4},{1,3},{3,1},{5,7},{7,5},{8,10},{10,8},{12,... | collective-permute-start | bytes 1572872 | tf_op jit(solution)/shard_map/ppermute | solution.py:25
  143.9 2.2 %slice-start.3 = ((s8[16777216]{0:T(1024)(128)(4,1)}), s8[4194304]{0:T(1024)(128)(4,1)S(1)}, s32[]{:S(2)}) async-start(s8[16777216]{0:T(1024)(128)(4,1)} %bitcast.24), calls=%async_computation.3 | async-start | bytes 8388608
  148.8 8.6 %collective-permute-start.25 = (bf16[64,2048]{1,0:T(8,128)(2,1)S(1)}, bf16[64,2048]{1,0:T(8,128)(2,1)S(1)}, u32[]{:S(2)}, u32[]{:S(2)}) collective-permute-start(bf16[64,2048]{1,0:T(8,128)(2,1)S(1)} %slice.204), channel_id=1, source_target_pairs={{0,1},{1,0},{2,3},{3,2},{4,5},{5,4},{6,7},{7,6},{8,9},{9,8},{10,11... | collective-permute-start | bytes 786440 | tf_op jit(solution)/shard_map/ppermute | solution.py:25
  156.8 7.5 %collective-permute-start.5 = (bf16[64,2048]{1,0:T(8,128)(2,1)S(1)}, bf16[64,2048]{1,0:T(8,128)(2,1)S(1)}, u32[]{:S(2)}, u32[]{:S(2)}) collective-permute-start(bf16[64,2048]{1,0:T(8,128)(2,1)S(1)} %slice.205), channel_id=1, source_target_pairs={{0,1},{1,0},{2,3},{3,2},{4,5},{5,4},{6,7},{7,6},{8,9},{9,8},{10,11... | collective-permute-start | bytes 786440 | tf_op jit(solution)/shard_map/ppermute | solution.py:25
